TPU v7x, 256 devices: a whole 4x4x8 slice. The times are simulated.
256 devices in a mesh: zero: 8 (over z), width: 16 (over y, x), unit: 2 (over core).
Axes of the slice: x: 4, y: 4, z: 8, core: 2. Of those that a mesh axis runs over, the one named last changes fastest.
Arguments:
- train_query: bfloat16 [8192, 4096], P(('unit', 'zero'), 'width'), parts along dimension 0, may hold values from -0.125 to 0.125
- low_query: bfloat16 [8192, 16], P(('unit', 'zero')), parts along dimension 0, may hold values from -0.09375 to 0.09375
- high_query: bfloat16 [32, 4096], P('unit', 'width'), parts along dimension 0, may hold values from -1.5 to 1.5
- train_key: bfloat16 [8192, 4096], P(('unit', 'zero'), 'width'), parts along dimension 0, may hold values from -0.125 to 0.125
- low_key: bfloat16 [8192, 16], P(('unit', 'zero')), parts along dimension 0, may hold values from -0.09375 to 0.09375
- high_key: bfloat16 [32, 4096], P('unit', 'width'), parts along dimension 0, may hold values from -1.5 to 1.5
- train_value: bfloat16 [8192, 4096], P(('unit', 'zero'), 'width'), parts along dimension 0, may hold values from -0.125 to 0.125
- low_value: bfloat16 [8192, 16], P(('unit', 'zero')), parts along dimension 0, may hold values from -0.09375 to 0.09375
- high_value: bfloat16 [32, 4096], P('unit', 'width'), parts along dimension 0, may hold values from -1.5 to 1.5
- norm_train: float32 [8192], P(('unit', 'zero', 'width')), parts along dimension 0, may hold values from 0.25 to 1.75
- norm_step: float32 [8192], P(('unit', 'zero', 'width')), parts along dimension 0, may hold values from -0.3 to 0.3
Outputs:
- serve_query: bfloat16 [8192, 4096], P('unit', 'width'), parts along dimension 0
- serve_key: bfloat16 [8192, 4096], P('unit', 'width'), parts along dimension 0
- serve_value: bfloat16 [8192, 4096], P('unit', 'width'), parts along dimension 0
- factor_query: float32 [8192], P(('unit', 'width')), parts along dimension 0
- factor_key: float32 [8192], P(('unit', 'width')), parts along dimension 0
- factor_value: float32 [8192], P(('unit', 'width')), parts along dimension 0
- serve_norm: bfloat16 [8192], P('unit'), parts along dimension 0
There are 2 independent parts, one for each index of `unit`. A program takes and returns all parts, laid end to end along the dimension named above; each array names one. Nothing has to cross between parts.
All inputs are finite; a program needn't handle non-finite values. Where the computation divides by a largest or mean magnitude, that divisor is 1e-20 or more.
Results may differ from a plain program's by a relative error of at most 0.001.
Values may be sent and summed in bfloat16 or wider, within the bound.
A program may use at most 64 MiB of HBM per device.

v0:
```python
import jax
import jax.numpy as jnp
from jax import lax
from jax.sharding import Mesh
from jax.sharding import PartitionSpec as P

ZERO_WIDTH = ("zero", "width_0", "width_1")
WIDTH = ("width_0", "width_1")
UNIT_ZERO_WIDTH = ("unit", "zero", "width_0", "width_1")
UNIT_WIDTH = ("unit", "width_0", "width_1")


mix_rate = 1.0


def copy_for_each(shard, axis):
    peers = lax.axis_size(axis)
    return lax.all_to_all(
        jnp.broadcast_to(shard[None], (peers, *shard.shape)), axis, 0, 0, tiled=True
    )


def of_everyone(shard, axis):
    everything = copy_for_each(shard, axis)
    return jnp.max(everything, axis=0)


def in_one(arrays, axis):
    vector, at, outs = (jnp.concatenate([a.reshape(-1) for a in arrays]), 0, [])
    so_far = of_everyone(vector, axis)
    for a in arrays:
        outs.append(so_far[at : at + a.size].reshape(a.shape))
        at += a.size
    return tuple(outs)


def sent_together(arrays, axis, dim, along):
    both = jnp.concatenate(arrays, axis=along)
    out, at, outs = (lax.all_gather(both, axis, axis=dim, tiled=True), 0, [])
    for a in arrays:
        outs.append(lax.slice_in_dim(out, at, at + a.shape[along], axis=along))
        at += a.shape[along]
    return tuple(outs)


def whole_of(shard, axes, dim):
    if not axes:
        return shard
    nearer = lax.all_gather(shard, axes[-1], axis=dim, tiled=True)
    return whole_of(nearer, axes[:-1], dim)


def per_device(
    train_query,
    low_query,
    high_query,
    train_key,
    low_key,
    high_key,
    train_value,
    low_value,
    high_value,
    norm_train,
    norm_step,
):
    fresh_query = train_query.astype(jnp.float32) + mix_rate * jnp.dot(
        low_query, high_query, preferred_element_type=jnp.float32
    )
    fresh_key = train_key.astype(jnp.float32) + mix_rate * jnp.dot(
        low_key, high_key, preferred_element_type=jnp.float32
    )
    fresh_value = train_value.astype(jnp.float32) + mix_rate * jnp.dot(
        low_value, high_value, preferred_element_type=jnp.float32
    )
    factor_query, factor_key, factor_value = in_one(
        (
            jnp.max(jnp.abs(fresh_query), axis=0),
            jnp.max(jnp.abs(fresh_key), axis=0),
            jnp.max(jnp.abs(fresh_value), axis=0),
        ),
        "zero",
    )
    narrow_query, narrow_key, narrow_value = (
        (fresh_query / factor_query).astype(jnp.bfloat16),
        (fresh_key / factor_key).astype(jnp.bfloat16),
        (fresh_value / factor_value).astype(jnp.bfloat16),
    )
    serve_query, serve_key, serve_value = sent_together(
        (narrow_query, narrow_key, narrow_value), "zero", 0, 1
    )
    serve_norm = whole_of((norm_train + norm_step).astype(jnp.bfloat16), ZERO_WIDTH, 0)
    return (serve_query, serve_key, serve_value, factor_query, factor_key, factor_value, serve_norm)


def solution(mesh):
    finer = Mesh(
        mesh.devices.reshape(mesh.shape["zero"], 4, 4, mesh.shape["unit"]),
        ("zero", "width_0", "width_1", "unit"),
    )
    placed = (
        P(("unit", "zero"), WIDTH),
        P(("unit", "zero"), None),
        P("unit", WIDTH),
        P(("unit", "zero"), WIDTH),
        P(("unit", "zero"), None),
        P("unit", WIDTH),
        P(("unit", "zero"), WIDTH),
        P(("unit", "zero"), None),
        P("unit", WIDTH),
        P(UNIT_ZERO_WIDTH),
        P(UNIT_ZERO_WIDTH),
    )
    return jax.shard_map(
        per_device,
        mesh=finer,
        in_specs=placed,
        out_specs=(
            P("unit", WIDTH),
            P("unit", WIDTH),
            P("unit", WIDTH),
            P(UNIT_WIDTH),
            P(UNIT_WIDTH),
            P(UNIT_WIDTH),
            P("unit"),
        ),
        check_vma=False,
    )
```

profile of v0, /device:TPU:2, one launch (start us, length us, event | category | flops | bytes accessed | tf_op | source)
XLA Modules:
  0.0 112.9 jit_solution(13729140163516430467)
XLA Ops:
  7.2 0.0 copy-start
  7.2 0.0 all-gather.4.cloned.1.call-start
  7.2 0.7 copy-done
  7.9 1.2 %abs_reduce_fusion = (f32[256]{0:T(256)S(1)}, f32[512,256]{1,0:T(8,128)S(1)}) fusion(bf16[512,16]{0,1:T(8,128)(2,1)S(1)} %copy-done, bf16[16,256]{1,0:T(8,128)(2,1)} %param.19, bf16[512,256]{1,0:T(8,128)(2,1)} %param.17), kind=kOutput, calls=%fused_computation.7 | convolution fusion | flops 4718336 | bytes 812032 | tf_op jit(solution)/shard_map/dot_general | solution.py:72
  9.1 1.3 %abs_reduce_fusion.1 = (f32[256]{0:T(256)S(1)}, f32[512,256]{1,0:T(8,128)S(1)}) fusion(bf16[512,16]{0,1:T(8,128)(2,1)} %param.15, bf16[16,256]{1,0:T(8,128)(2,1)} %param.16, bf16[512,256]{1,0:T(8,128)(2,1)} %param.14), kind=kOutput, calls=%fused_computation.8 | convolution fusion | flops 4718336 | bytes 812032 | tf_op jit(solution)/shard_map/dot_general | solution.py:69
  10.4 1.3 %abs_reduce_fusion.2 = (f32[256]{0:T(256)S(1)}, f32[512,256]{1,0:T(8,128)S(1)}) fusion(bf16[512,16]{0,1:T(8,128)(2,1)} %param.12, bf16[16,256]{1,0:T(8,128)(2,1)} %param.13, bf16[512,256]{1,0:T(8,128)(2,1)} %param.11), kind=kOutput, calls=%fused_computation.9 | convolution fusion | flops 4718336 | bytes 812032 | tf_op jit(solution)/shard_map/dot_general | solution.py:66
  11.7 16.1 %all_to_all.6 = f32[8,1,768]{2,1,0:T(1,128)S(1)} all-to-all(f32[8,1,768]{2,1,0:T(1,128)S(1)} %broadcast_in_dim.2), channel_id=1, replica_groups=mesh['zero'=8,'width_0'=4,'width_1'=4,'unit'=2] {'zero'}, dimensions={0} | all-to-all | bytes 49152 | tf_op jit(solution)/shard_map/all_to_all | solution.py:18
  27.8 0.0 copy-start.1
  27.8 0.0 copy-start.2
  27.8 0.0 copy-start.3
  27.9 0.0 copy-start.6
  27.9 0.0 copy-start.4
  27.9 0.0 copy-start.5
  27.9 0.1 divide_convert_fusion
  28.0 0.9 pad_maximum_fusion
  29.0 0.0 all-gather.4.cloned.1.call-update
  29.0 0.0 copy-done.1
  29.0 0.0 copy-done.2
  29.0 0.0 copy-done.3
  29.0 0.0 copy-done.6
  29.0 0.6 dynamic-slice
  30.3 0.0 copy-done.4
  30.3 0.0 copy-done.5
  30.3 0.2 dynamic-update-slice
  30.6 8.6 %all-reduce = bf16[128]{0:T(256)(128)(2,1)S(1)} all-reduce(bf16[128]{0:T(256)(128)(2,1)S(1)} %dynamic-update-slice), channel_id=1, replica_groups=mesh['zero'=8,'width_0'=4,'width_1'=4,'unit'=2] {'width_1'}, use_global_device_ids=true, to_apply=%add | all-reduce | flops 128 | bytes 512
  39.2 10.0 %all-gather = bf16[4,1,128]{2,1,0:T(2,128)(2,1)S(1)} all-gather(bf16[1,1,128]{2,1,0:T(2,128)(2,1)S(1)} %bitcast.14), channel_id=1, replica_groups=mesh['zero'=8,'width_0'=4,'width_1'=4,'unit'=2] {'width_0'}, dimensions={0}, use_global_device_ids=true | all-gather | bytes 1280 | tf_op jit(solution)/shard_map/all_gather | solution.py:49
  49.1 21.8 %all-gather.1 = bf16[8,1,512]{2,1,0:T(2,128)(2,1)S(1)} all-gather(bf16[1,1,512]{2,1,0:T(2,128)(2,1)S(1)} %bitcast.12), channel_id=1, replica_groups=mesh['zero'=8,'width_0'=4,'width_1'=4,'unit'=2] {'zero'}, dimensions={0}, use_global_device_ids=true | all-gather | bytes 9216 | tf_op jit(solution)/shard_map/all_gather | solution.py:49
  71.0 0.6 copy.24
  71.6 28.8 %all-gather.4.cloned.1.call-done = bf16[4096,768]{1,0:T(8,128)(2,1)} async-done(((bf16[512,768]{1,0:T(8,128)(2,1)}), bf16[4096,768]{1,0:T(8,128)(2,1)}) %all-gather.4.cloned.1.call-update) | async-done | bytes 6291472 | tf_op jit(solution)/shard_map/all_gather | solution.py:39
  100.3 5.7 %fusion = (bf16[4096,256]{1,0:T(8,128)(2,1)}, bf16[4096,256]{1,0:T(8,128)(2,1)}, bf16[4096,256]{1,0:T(8,128)(2,1)}) fusion(bf16[4096,768]{1,0:T(8,128)(2,1)} %all-gather.4.cloned.1.call-done), kind=kLoop, calls=%fused_computation.12 | loop fusion | bytes 12582912 | tf_op jit(solution)/shard_map/slice | solution.py:41
  (8 shorter events, 0.2 us)
Async XLA Ops:
  7.2 0.7 copy-start
  7.2 93.1 %all-gather.4.cloned.1.call-start = ((), (), s32[]{:S(2)}) async-start(), calls=%async_computation.1 | async-start | bytes 7077888 | tf_op jit(solution)/shard_map/all_gather | solution.py:39
  27.8 1.2 %copy-start.1 = (f32[256]{0:T(256)}, f32[256]{0:T(256)S(1)}, u32[]{:S(2)}) copy-start(f32[256]{0:T(256)S(1)} %get-tuple-element.10) | copy-start | bytes 3076
  27.8 1.2 %copy-start.2 = (f32[256]{0:T(256)}, f32[256]{0:T(256)S(1)}, u32[]{:S(2)}) copy-start(f32[256]{0:T(256)S(1)} %get-tuple-element.11) | copy-start | bytes 3076
  27.8 1.2 %copy-start.3 = (f32[256]{0:T(256)}, f32[256]{0:T(256)S(1)}, u32[]{:S(2)}) copy-start(f32[256]{0:T(256)S(1)} %get-tuple-element.12) | copy-start | bytes 3076
  27.9 1.1 copy-start.6
  27.9 2.4 %copy-start.4 = (f32[32]{0:T(128)S(1)}, f32[32]{0:T(128)}, u32[]{:S(2)}) copy-start(f32[32]{0:T(128)} %param.20) | copy-start | bytes 388
  27.9 2.4 %copy-start.5 = (f32[32]{0:T(128)S(1)}, f32[32]{0:T(128)}, u32[]{:S(2)}) copy-start(f32[32]{0:T(128)} %param.21) | copy-start | bytes 388
Sparse Core Ops, SparseCore 0:
  29.1 71.1 all-gather.3
where the time goes:
time: 114 us; the launch traced here: 113 us
  blocking collectives  56.4 us (49%)
  waiting for transfers between devices  28.8 us (25%)
  between operations  14.9 us (13%)
  local copies, waits for them, and re-layouts  7.89 us (7%)
  matrix products  3.75 us (3%)
  other arithmetic  1.16 us (1%)
    all_gather x2, blocking collectives, whole_of(): nearer = lax.all_gather(shard, axes[-1], axis=dim, tiled=True)  31.7 us
    all_gather x1, waiting for transfers between devices, sent_together(): out, at, outs = (lax.all_gather(both, axis, axis=dim, tiled=True), 0, [])  28.8 us
    all_to_all x1, blocking collectives, copy_for_each(): lax.all_to_all(jnp.broadcast_to(shard[None], (peers, *shard.shape)), axis...  16.1 us
    unnamed x1, blocking collectives  8.59 us
    slice x1, local copies, waits for them, and re-layouts, sent_together(): outs.append(lax.slice_in_dim(out, at, at + a.shape[along], axis=along))  5.72 us
  transfers between devices with their start and end apart: 1, of which 1 were waited for; matrix products, arithmetic and copies ran while one was open for 1% of the time, Pallas kernels for 0%

commit v1 on v0

v1 whole, which is shorter than its diff:
```python
import functools

import jax
import jax.numpy as jnp
from jax import lax
from jax.experimental import pallas as pl
from jax.experimental.pallas import tpu as pltpu
from jax.sharding import Mesh
from jax.sharding import PartitionSpec as P

WIDTH = ("width_0", "width_1")
UNIT_ZERO_WIDTH = ("unit", "zero", "width_0", "width_1")
UNIT_WIDTH = ("unit", "width_0", "width_1")
MESH = pl.DeviceIdType.MESH

mix_rate = 1.0

Z = 8
ROWS = 512
COLS = 256
WHOLE = Z * ROWS
BLOCK = 128
RAW = 384
PIECE = 64
NRAW = RAW // PIECE
NBLOCK = 3 * ROWS // BLOCK
FIRST = RAW // BLOCK
META = 3 * COLS + 128


def fresh_of(low_t, high, train):
    product = lax.dot_general(
        low_t, high, (((0,), (0,)), ((), ())), preferred_element_type=jnp.float32
    )
    return train.astype(jnp.float32) + mix_rate * product


def gather_kernel(
    tq, lq, hq, tk, lk, hk, tv, lv, hv, nt, ns,
    out, factors, norm,
    train, low, high, norm_in, fresh, rawx, lowx, meta, norm_x, norm_y, inverse,
    load_sem, raw_s, raw_r, blk_s, blk_r, meta_s, meta_r, low_s, low_r, nx_s, nx_r, ny_s, ny_r,
):
    z = lax.axis_index("zero")
    y = lax.axis_index("width_0")
    x = lax.axis_index("width_1")

    loads = [
        pltpu.make_async_copy(tq, train.at[0], load_sem.at[0]),
        pltpu.make_async_copy(lq, low.at[0], load_sem.at[1]),
        pltpu.make_async_copy(hq, high.at[0], load_sem.at[2]),
        pltpu.make_async_copy(tk, train.at[1], load_sem.at[3]),
        pltpu.make_async_copy(lk, low.at[1], load_sem.at[4]),
        pltpu.make_async_copy(hk, high.at[1], load_sem.at[5]),
        pltpu.make_async_copy(tv, train.at[2], load_sem.at[6]),
        pltpu.make_async_copy(lv, low.at[2], load_sem.at[7]),
        pltpu.make_async_copy(hv, high.at[2], load_sem.at[8]),
        pltpu.make_async_copy(nt, norm_in.at[0], load_sem.at[9]),
        pltpu.make_async_copy(ns, norm_in.at[1], load_sem.at[10]),
    ]
    for load in loads:
        load.start()

    def beside(axis, at, step, size):
        return {axis: lax.rem(at + (step + size), size)}

    towards = (beside("zero", z, 1, Z), beside("zero", z, -1, Z))
    barrier = pltpu.get_barrier_semaphore()
    neighbours = towards + (
        beside("width_0", y, 1, 4), beside("width_0", y, -1, 4),
        beside("width_1", x, 1, 4), beside("width_1", x, -1, 4),
    )
    for neighbour in neighbours:
        pl.semaphore_signal(barrier, inc=1, device_id=neighbour, device_id_type=MESH)
    pl.semaphore_wait(barrier, len(neighbours))

    def origin(d, h):
        back = h - 1
        return lax.rem(z + (Z - back if d == 0 else back), Z)

    def remote(src, dst, send, recv, d):
        return pltpu.make_async_remote_copy(
            src_ref=src, dst_ref=dst, send_sem=send, recv_sem=recv,
            device_id=towards[d], device_id_type=MESH,
        )

    def half(start, size, d, h):
        return (start, size) if h < 4 else (start + d * (size // 2), size // 2)

    def raw_copy(d, h, c):
        at, size = half(c * PIECE, PIECE, d, h)
        o = origin(d, h)
        there = rawx.at[o, pl.ds(at, size)]
        here = train.at[0, pl.ds(at, size)] if h == 1 else there
        return remote(here, there, raw_s.at[d, h - 1, c], raw_r.at[d, h - 1, c], d)

    def low_copy(d, h):
        o = origin(d, h)
        there = lowx.at[o]
        here = low.at[0, :, pl.ds(0, RAW)] if h == 1 else there
        return remote(here, there, low_s.at[d, h - 1], low_r.at[d, h - 1], d)

    def meta_copy(d, h):
        o = origin(d, h)
        return remote(meta.at[o], meta.at[o], meta_s.at[d, h - 1], meta_r.at[d, h - 1], d)

    def row_of(j, o):
        return (j // 4) * WHOLE + o * ROWS + (j % 4) * BLOCK

    def block_copy(d, h, j):
        at, size = half(row_of(j, origin(d, h)), BLOCK, d, h)
        ref = out.at[pl.ds(pl.multiple_of(at, size), size)]
        return remote(ref, ref, blk_s.at[d, h - 1, j], blk_r.at[d, h - 1, j], d)

    def copies(item, h):
        if item == "meta":
            return [meta_copy(d, h) for d in ((0, 1) if h < 4 else (0,))]
        if item == "low":
            return [low_copy(d, h) for d in ((0, 1) if h < 4 else (1,))]
        return [raw_copy(d, h, item) for d in (0, 1)]

    queue = []
    sent = set()

    def left(n):
        for entry in queue[: max(0, len(queue) - n)]:
            if entry not in sent:
                sent.add(entry)
                for copy in copies(*entry):
                    copy.wait_send()

    def send(item, h, depth=3):
        left(depth - 1)
        if h > 1:
            arrived(item, h - 1)
        for copy in copies(item, h):
            copy.start()
        queue.append((item, h))

    landed = set()

    def arrived(item, h):
        if (item, h) not in landed:
            landed.add((item, h))
            for copy in copies(item, h):
                copy.wait_recv()

    loads[0].wait()
    send(0, 1)
    send(1, 1)
    for load in loads[1:]:
        load.wait()
    for m in range(3):
        top = jnp.zeros((8, COLS), jnp.float32)
        for b in range(ROWS // BLOCK):
            rows = pl.ds(b * BLOCK, BLOCK)
            block = fresh_of(low[m, :, rows], high[m], train[m, rows])
            fresh[m, rows] = block
            top = jnp.maximum(top, jnp.max(jnp.abs(block).reshape(BLOCK // 8, 8, COLS), axis=0))
        meta[z, :, pl.ds(m * COLS, COLS)] = jnp.max(top, axis=0, keepdims=True)
    gain = (norm_in[0] + norm_in[1]).astype(jnp.bfloat16)
    lane = lax.broadcasted_iota(jnp.int32, (32, 128), 1)
    entry = lax.broadcasted_iota(jnp.int32, (32, 128), 0)
    place = (lane == entry + 32 * x).astype(jnp.bfloat16)
    meta[z, :, pl.ds(3 * COLS, 128)] = jnp.dot(gain, place, preferred_element_type=jnp.float32)

    order = [
        ("meta", 1), (2, 1), (3, 1), (4, 1), ("meta", 2), (5, 1), ("low", 1), (0, 2), (1, 2),
        ("meta", 3), (2, 2), (3, 2), (4, 2), ("meta", 4), (5, 2), ("low", 2), (0, 3), (1, 3), (2, 3), (3, 3),
    ]
    for item, h in order:
        send(item, h)
    arrived("meta", 4)

    top = jnp.max(meta[:, 0, : 3 * COLS], axis=0, keepdims=True)
    for m in range(3):
        factors[pl.ds(m, 1)] = top[:, m * COLS : (m + 1) * COLS]
        inverse[m] = 1.0 / top[:, m * COLS : (m + 1) * COLS]

    def scale_own(j):
        m, r = j // 4, (j % 4) * BLOCK
        scaled = fresh[m, pl.ds(r, BLOCK)] * inverse[m]
        out[pl.ds(pl.multiple_of(row_of(j, z), BLOCK), BLOCK)] = scaled.astype(jnp.bfloat16)

    for j in range(FIRST, NBLOCK):
        scale_own(j)
        if j >= FIRST + 1:
            for d in (0, 1):
                block_copy(d, 1, j - 1).start()
    for j in range(FIRST):
        scale_own(j)
    for d in (0, 1):
        block_copy(d, 1, NBLOCK - 1).start()

    for item, h in [(4, 3), (5, 3), ("low", 3)] + [(c, 4) for c in range(NRAW)] + [("low", 4)]:
        send(item, h, depth=64)

    def pass_round(buf, at, axis, send_sem, recv_sem):
        def hop(n, slot, step):
            slot = lax.rem(at + slot + 4, 4)
            return pltpu.make_async_remote_copy(
                src_ref=buf.at[slot], dst_ref=buf.at[slot], send_sem=send_sem.at[n],
                recv_sem=recv_sem.at[n], device_id=beside(axis, at, step, 4), device_id_type=MESH,
            )
        hop(0, 0, 1).start()
        hop(1, 0, -1).start()
        hop(0, 0, 1).wait_recv()
        hop(2, -1, 1).start()
        hop(1, 0, -1).wait_recv()
        hop(2, -1, 1).wait_recv()
        for n, slot, step in ((0, 0, 1), (1, 0, -1), (2, -1, 1)):
            hop(n, slot, step).wait_send()

    norm_x[x] = meta[:, 0, 3 * COLS :]
    pass_round(norm_x, x, "width_1", nx_s, nx_r)
    norm_y[y] = jnp.sum(norm_x[...], axis=0)
    pass_round(norm_y, y, "width_0", ny_s, ny_r)
    for s in range(4):
        norm[s] = norm_y[s]

    def scale_raw(o):
        for j in range(FIRST):
            rows = pl.ds(j * BLOCK, BLOCK)
            block = fresh_of(lowx[o, :, rows], high[0], rawx[o, rows])
            at = pl.multiple_of(row_of(j, o), BLOCK)
            out[pl.ds(at, BLOCK)] = (block * inverse[0]).astype(jnp.bfloat16)

    for h in (1, 2, 3):
        for c in range(NRAW):
            arrived(c, h)
        arrived("low", h)
        scale_raw(lax.rem(z + Z - h, Z))
        scale_raw(lax.rem(z + h, Z))

    for h in (1, 2, 3):
        def forward(j, _, h=h):
            for d in (0, 1):
                block_copy(d, h, j).wait_recv()
                block_copy(d, h + 1, j).start()
            return 0
        lax.fori_loop(FIRST, NBLOCK, forward, 0)
        if h == 2:
            for c in range(NRAW):
                arrived(c, 4)
            arrived("low", 4)
            scale_raw(lax.rem(z + 4, Z))

    def finish(j, _):
        for d in (0, 1):
            block_copy(d, 4, j).wait_recv()
        return 0
    lax.fori_loop(FIRST, NBLOCK, finish, 0)

    def drain(j, _):
        for h in (1, 2, 3, 4):
            for d in (0, 1):
                block_copy(d, h, j).wait_send()
        return 0
    lax.fori_loop(FIRST, NBLOCK, drain, 0)
    left(0)


def write_kernel(weights, factors, norm, sq, sk, sv, fq, fk, fv, gain, sem):
    outs = (sq, sk, sv)
    writes = [
        pltpu.make_async_copy(weights.at[pl.ds(m * WHOLE, WHOLE)], outs[m], sem.at[m])
        for m in range(3)
    ]
    for write in writes:
        write.start()
    for m, ref in enumerate((fq, fk, fv)):
        ref[...] = factors[m]
    for z in range(Z):
        for y in range(4):
            gain[pl.ds(z * 4 + y, 1)] = norm[y, pl.ds(z, 1)].astype(jnp.bfloat16)
    for write in writes:
        write.wait()


def per_device(tq, lq, hq, tk, lk, hk, tv, lv, hv, nt, ns):
    hbm = pl.BlockSpec(memory_space=pl.ANY)
    vmem = pl.BlockSpec(memory_space=pltpu.VMEM)
    dma = pltpu.SemaphoreType.DMA
    f32, bf16 = jnp.float32, jnp.bfloat16
    weights, factors, norm = pl.pallas_call(
        gather_kernel,
        name="gather_z",
        out_shape=(
            pltpu.VMEM((3 * WHOLE, COLS), bf16),
            pltpu.VMEM((8, COLS), f32),
            pltpu.VMEM((4, Z, 128), f32),
        ),
        in_specs=[hbm] * 11,
        out_specs=(vmem, vmem, vmem),
        scratch_shapes=[
            pltpu.VMEM((3, ROWS, COLS), bf16),
            pltpu.VMEM((3, 16, ROWS), bf16),
            pltpu.VMEM((3, 16, COLS), bf16),
            pltpu.VMEM((2, 1, 32), f32),
            pltpu.VMEM((3, ROWS, COLS), f32),
            pltpu.VMEM((Z, RAW, COLS), bf16),
            pltpu.VMEM((Z, 16, RAW), bf16),
            pltpu.VMEM((Z, 1, META), f32),
            pltpu.VMEM((4, Z, 128), f32),
            pltpu.VMEM((4, Z, 128), f32),
            pltpu.VMEM((3, 1, COLS), f32),
            dma((11,)),
            dma((2, 4, NRAW)), dma((2, 4, NRAW)),
            dma((2, 4, NBLOCK)), dma((2, 4, NBLOCK)),
            dma((2, 4)), dma((2, 4)), dma((2, 4)), dma((2, 4)),
            dma((3,)), dma((3,)), dma((3,)), dma((3,)),
        ],
        compiler_params=pltpu.CompilerParams(
            collective_id=0, has_side_effects=True, vmem_limit_bytes=32 * 1024 * 1024
        ),
    )(tq, lq.T, hq, tk, lk.T, hk, tv, lv.T, hv, nt.reshape(1, 32), ns.reshape(1, 32))
    sq, sk, sv, fq, fk, fv, gain = pl.pallas_call(
        write_kernel,
        name="write_out",
        out_shape=(
            jax.ShapeDtypeStruct((WHOLE, COLS), bf16),
            jax.ShapeDtypeStruct((WHOLE, COLS), bf16),
            jax.ShapeDtypeStruct((WHOLE, COLS), bf16),
            jax.ShapeDtypeStruct((COLS,), f32),
            jax.ShapeDtypeStruct((COLS,), f32),
            jax.ShapeDtypeStruct((COLS,), f32),
            jax.ShapeDtypeStruct((32, 128), bf16),
        ),
        in_specs=[vmem] * 3,
        out_specs=(hbm, hbm, hbm, vmem, vmem, vmem, vmem),
        scratch_shapes=[dma((3,))],
        compiler_params=pltpu.CompilerParams(vmem_limit_bytes=16 * 1024 * 1024),
    )(weights, factors, norm)
    return sq, sk, sv, fq, fk, fv, gain.reshape(4096)


def solution(mesh):
    finer = Mesh(
        mesh.devices.reshape(mesh.shape["zero"], 4, 4, mesh.shape["unit"]),
        ("zero", "width_0", "width_1", "unit"),
    )
    matrix, low, high = P(("unit", "zero"), WIDTH), P(("unit", "zero"), None), P("unit", WIDTH)
    return jax.shard_map(
        per_device,
        mesh=finer,
        in_specs=(matrix, low, high) * 3 + (P(UNIT_ZERO_WIDTH), P(UNIT_ZERO_WIDTH)),
        out_specs=(high, high, high, P(UNIT_WIDTH), P(UNIT_WIDTH), P(UNIT_WIDTH), P("unit")),
        check_vma=False,
    )
```

time: 114 us -> 93.5 us (0.82)
  Pallas kernels: 0 us -> 83.8 us
  blocking collectives: 56.4 us -> 0 us
  waiting for transfers between devices: 28.8 us -> 0 us
  between operations: 14.9 us -> 0.66 us
  matrix products: 3.75 us -> 0 us
  other arithmetic: 1.16 us -> 0 us
    pallas_call x0 -> x2, Pallas kernels: none -> 83.8 us  [the longest x1 80.5 us: per_device(): pl.pallas_call(gather_kernel, name='gather_z', out_shape=(pltpu.VMEM((3 *...]
    all_gather x2 -> x0, blocking collectives: 31.7 us -> none  [whole_of(): nearer = lax.all_gather(shard, axes[-1], axis=dim, tiled=True)]
    all_gather x1 -> x0, waiting for transfers between devices: 28.8 us -> none  [sent_together(): out, at, outs = (lax.all_gather(both, axis, axis=dim, tiled=True), 0, [])]
    all_to_all x1 -> x0, blocking collectives: 16.1 us -> none  [copy_for_each(): lax.all_to_all(jnp.broadcast_to(shard[None], (peers, *shard.shape)), axis...]
    unnamed x1 -> x0, blocking collectives: 8.59 us -> none
    unnamed x18 -> x22, local copies, waits for them, and re-layouts: 2.15 us -> 8.39 us
    slice x2 -> x0, local copies, waits for them, and re-layouts: 5.73 us -> none  [the longest x1 5.72 us: sent_together(): outs.append(lax.slice_in_dim(out, at, at + a.shape[along], axis=along))]
    dot_general x3 -> x0, matrix products: 3.75 us -> none  [the longest x1 1.26 us: per_device(): jnp.dot(low_key, high_key, preferred_element_type=jnp.float32)]
  transfers between devices with their start and end apart: 1 -> 0, of which waited for: 1 -> 0; matrix products, arithmetic and copies ran while one was open for 1% -> 0% of each run, Pallas kernels for 0% -> 0%
where the time goes in v1:
time: 93.5 us; the launch traced here: 92.9 us
  Pallas kernels  83.8 us (90%)
  local copies, waits for them, and re-layouts  8.39 us (9%)
    pallas_call x1, Pallas kernels, per_device(): pl.pallas_call(gather_kernel, name='gather_z', out_shape=(pltpu.VMEM((3 *...  80.5 us
    unnamed x22, local copies, waits for them, and re-layouts  8.39 us
    pallas_call x1, Pallas kernels, per_device(): pl.pallas_call(write_kernel, name='write_out', out_shape=(jax.ShapeDtypeS...  3.34 us

profile of v1, /device:TPU:2, one launch (start us, length us, event | category | flops | bytes accessed | tf_op | source)
XLA Modules:
  0.0 92.9 jit_solution(1807952611951394668)
XLA Ops:
  0.6 0.0 copy-start
  0.6 0.9 %copy-done = bf16[512,256]{1,0:T(8,128)(2,1)S(1)} copy-done((bf16[512,256]{1,0:T(8,128)(2,1)S(1)}, bf16[512,256]{1,0:T(8,128)(2,1)}, u32[]{:S(2)}) %copy-start) | copy-done | bytes 262168
  1.6 0.0 copy-start.1
  1.6 0.9 %copy-done.1 = bf16[512,256]{1,0:T(8,128)(2,1)S(1)} copy-done((bf16[512,256]{1,0:T(8,128)(2,1)S(1)}, bf16[512,256]{1,0:T(8,128)(2,1)}, u32[]{:S(2)}) %copy-start.1) | copy-done | bytes 262168
  2.5 0.0 copy-start.2
  2.5 0.9 %copy-done.2 = bf16[512,256]{1,0:T(8,128)(2,1)S(1)} copy-done((bf16[512,256]{1,0:T(8,128)(2,1)S(1)}, bf16[512,256]{1,0:T(8,128)(2,1)}, u32[]{:S(2)}) %copy-start.2) | copy-done | bytes 262168
  3.5 0.0 copy-start.3
  3.5 0.7 copy-done.3
  4.2 0.0 copy-start.4
  4.2 0.7 copy-done.4
  4.9 0.0 copy-start.5
  4.9 0.7 copy-done.5
  5.6 0.0 copy-start.6
  5.6 0.7 copy-done.6
  6.3 0.0 copy-start.7
  6.3 0.7 copy-done.7
  7.0 0.0 copy-start.8
  7.0 0.7 copy-done.8
  7.7 0.0 copy-start.9
  7.7 0.7 copy-done.9
  8.4 0.0 copy-start.10
  8.4 0.7 copy-done.10
  9.0 80.5 %gather_z.1 = (bf16[12288,256]{1,0:T(8,128)(2,1)S(1)}, f32[8,256]{1,0:T(8,128)S(1)}, f32[4,8,128]{2,1,0:T(8,128)S(1)}) custom-call(bf16[512,256]{1,0:T(8,128)(2,1)S(1)} %copy-done, bf16[16,512]{1,0:T(8,128)(2,1)S(1)} %bitcast.6, bf16[16,256]{1,0:T(8,128)(2,1)S(1)} %copy-done.6, bf16[512,256]{1,0:T(8,128)(2,1)S(1)} %copy-done.1, bf16[16,512]{1,0:T(8,128)(2,1)S(1)} %bitcast.7, ...), custom_call_target="tpu_custom_call" | custom-call | tf_op jit(solution)/shard_map/gather_z/pallas_call | solution.py:285
  89.5 3.3 %write_out.1 = (bf16[4096,256]{1,0:T(8,128)(2,1)}, bf16[4096,256]{1,0:T(8,128)(2,1)}, bf16[4096,256]{1,0:T(8,128)(2,1)}, f32[256]{0:T(256)}, f32[256]{0:T(256)}, /*index=5*/f32[256]{0:T(256)}, bf16[32,128]{1,0:T(8,128)(2,1)}) custom-call(bf16[12288,256]{1,0:T(8,128)(2,1)S(1)} %get-tuple-element.17.weights, f32[8,256]{1,0:T(8,128)S(1)} %get-tuple-element.18.factors, ...), custom_call_target="tpu_custom_call" | custom-call | tf_op jit(solution)/shard_map/write_out/pallas_call | solution.py:317
Async XLA Ops:
  0.6 1.0 %copy-start = (bf16[512,256]{1,0:T(8,128)(2,1)S(1)}, bf16[512,256]{1,0:T(8,128)(2,1)}, u32[]{:S(2)}) copy-start(bf16[512,256]{1,0:T(8,128)(2,1)} %tq.1) | copy-start | bytes 786436
  1.6 0.9 %copy-start.1 = (bf16[512,256]{1,0:T(8,128)(2,1)S(1)}, bf16[512,256]{1,0:T(8,128)(2,1)}, u32[]{:S(2)}) copy-start(bf16[512,256]{1,0:T(8,128)(2,1)} %tk.1) | copy-start | bytes 786436
  2.5 0.9 %copy-start.2 = (bf16[512,256]{1,0:T(8,128)(2,1)S(1)}, bf16[512,256]{1,0:T(8,128)(2,1)}, u32[]{:S(2)}) copy-start(bf16[512,256]{1,0:T(8,128)(2,1)} %tv.1) | copy-start | bytes 786436
  3.5 0.7 copy-start.3
  4.2 0.7 copy-start.4
  4.9 0.7 copy-start.5
  5.6 0.7 copy-start.6
  6.3 0.7 copy-start.7
  7.0 0.7 copy-start.8
  7.7 0.7 copy-start.9
  8.4 0.7 copy-start.10

commit v2 on v1

v2 whole, which is shorter than its diff:
```python
import functools

import jax
import jax.numpy as jnp
from jax import lax
from jax.experimental import pallas as pl
from jax.experimental.pallas import tpu as pltpu
from jax.sharding import Mesh
from jax.sharding import PartitionSpec as P

WIDTH = ("width_0", "width_1")
UNIT_ZERO_WIDTH = ("unit", "zero", "width_0", "width_1")
UNIT_WIDTH = ("unit", "width_0", "width_1")
MESH = pl.DeviceIdType.MESH

mix_rate = 1.0

Z = 8
ROWS = 512
COLS = 256
WHOLE = Z * ROWS
BLOCK = 128
NRAW = ROWS // BLOCK
PIECE = 256
NPIECE = 2 * ROWS // PIECE
META = 3 * COLS + 128


def fresh_of(low_t, high, train):
    product = lax.dot_general(
        low_t, high, (((0,), (0,)), ((), ())), preferred_element_type=jnp.float32
    )
    return train.astype(jnp.float32) + mix_rate * product


def gather_kernel(
    tq, lq, hq, tk, lk, hk, tv, lv, hv, nt, ns,
    out, factor_q, factor_k, factor_v, norm,
    train, low, high, norm_in, fresh, rawx, lowx, meta, norm_x, norm_y, norm_all, inverse,
    load_sem, raw_s, raw_r, piece_s, piece_r, meta_s, meta_r, low_s, low_r,
    lx_s, lx_r, nx_s, nx_r, ny_s, ny_r,
):
    z = lax.axis_index("zero")
    y = lax.axis_index("width_0")
    x = lax.axis_index("width_1")

    lanes = pl.ds(pl.multiple_of(x * BLOCK, BLOCK), BLOCK)
    loads = [
        pltpu.make_async_copy(src, dst, load_sem.at[n])
        for n, (src, dst) in enumerate((
            (tq, train.at[0]), (lq.at[:, lanes], lowx.at[x, z]), (lq, low.at[0]), (hq, high.at[0]),
            (tk, train.at[1]), (lk, low.at[1]), (hk, high.at[1]),
            (tv, train.at[2]), (lv, low.at[2]), (hv, high.at[2]),
            (nt, norm_in.at[0]), (ns, norm_in.at[1]),
        ))
    ]
    for load in loads:
        load.start()

    def beside(axis, at, step, size):
        return {axis: lax.rem(at + (step + size), size)}

    towards = (beside("zero", z, 1, Z), beside("zero", z, -1, Z))
    barrier = pltpu.get_barrier_semaphore()
    neighbours = towards + (
        beside("width_0", y, 1, 4), beside("width_0", y, -1, 4),
        beside("width_1", x, 1, 4), beside("width_1", x, -1, 4),
    )
    for neighbour in neighbours:
        pl.semaphore_signal(barrier, inc=1, device_id=neighbour, device_id_type=MESH)
    pl.semaphore_wait(barrier, len(neighbours))

    def origin(d, h):
        back = h - 1
        return lax.rem(z + (Z - back if d == 0 else back), Z)

    def remote(src, dst, send, recv, d):
        return pltpu.make_async_remote_copy(
            src_ref=src, dst_ref=dst, send_sem=send, recv_sem=recv,
            device_id=towards[d], device_id_type=MESH,
        )

    def half(start, size, d, h):
        return (start, size) if h < 4 else (start + d * (size // 2), size // 2)

    def raw_copy(d, h, c):
        at, size = half(c * BLOCK, BLOCK, d, h)
        there = rawx.at[origin(d, h), pl.ds(at, size)]
        here = train.at[0, pl.ds(at, size)] if h == 1 else there
        return remote(here, there, raw_s.at[d, h - 1, c], raw_r.at[d, h - 1, c], d)

    def low_copy(d, h):
        ref = lowx.at[x, origin(d, h)]
        return remote(ref, ref, low_s.at[d, h - 1], low_r.at[d, h - 1], d)

    def meta_copy(d, h):
        ref = meta.at[origin(d, h)]
        return remote(ref, ref, meta_s.at[d, h - 1], meta_r.at[d, h - 1], d)

    def row_of(m, r, o):
        return m * WHOLE + o * ROWS + r

    def piece_copy(d, h, j):
        m, r = 1 + j * PIECE // ROWS, j * PIECE % ROWS
        at, size = half(row_of(m, r, origin(d, h)), PIECE, d, h)
        ref = out.at[pl.ds(pl.multiple_of(at, size), size)]
        return remote(ref, ref, piece_s.at[d, h - 1, j], piece_r.at[d, h - 1, j], d)

    def copies(kind, n, h):
        if kind == "meta":
            return [meta_copy(d, h) for d in ((0, 1) if h < 4 else (0,))]
        if kind == "low":
            return [low_copy(d, h) for d in ((0, 1) if h < 4 else (1,))]
        return [(raw_copy if kind == "raw" else piece_copy)(d, h, n) for d in (0, 1)]

    sent, landed = [], set()

    def arrived(*item):
        if item not in landed:
            landed.add(item)
            for copy in copies(*item):
                copy.wait_recv()

    def send(*items):
        for kind, n, h in items:
            if h > 1:
                arrived(kind, n, h - 1)
            for copy in copies(kind, n, h):
                copy.start()
            sent.append((kind, n, h))

    def raw(h, *pieces):
        return [("raw", c, h) for c in pieces]

    def small(h):
        return [("low", 0, h), ("meta", 0, h)]

    loads[0].wait()
    loads[1].wait()
    send(("raw", 0, 1), ("low", 0, 1), ("raw", 1, 1))
    for load in loads[2:]:
        load.wait()
    for m in range(3):
        top = jnp.zeros((8, COLS), jnp.float32)
        for b in range(ROWS // BLOCK):
            rows = pl.ds(b * BLOCK, BLOCK)
            block = fresh_of(low[m, :, rows], high[m], train[m, rows])
            fresh[m, rows] = block
            top = jnp.maximum(top, jnp.max(jnp.abs(block).reshape(BLOCK // 8, 8, COLS), axis=0))
        meta[z, :, pl.ds(m * COLS, COLS)] = jnp.max(top, axis=0, keepdims=True)
    gain = (norm_in[0] + norm_in[1]).astype(jnp.bfloat16)
    lane = lax.broadcasted_iota(jnp.int32, (32, 128), 1)
    entry = lax.broadcasted_iota(jnp.int32, (32, 128), 0)
    place = (lane == entry + 32 * x).astype(jnp.bfloat16)
    meta[z, :, pl.ds(3 * COLS, 128)] = jnp.dot(gain, place, preferred_element_type=jnp.float32)

    send(("meta", 0, 1), *raw(1, 2, 3))
    send(*small(2), *raw(2, 0, 1))
    send(*small(3), *raw(2, 2, 3))
    send(*small(4), *raw(3, 0, 1, 2, 3))
    arrived("meta", 0, 4)

    top = jnp.max(meta[:, 0, : 3 * COLS], axis=0, keepdims=True)
    for m, factor in enumerate((factor_q, factor_k, factor_v)):
        of_m = top[:, m * COLS : (m + 1) * COLS]
        factor[...] = of_m[0]
        inverse[m] = 1.0 / of_m

    def scale_own(m, r, size):
        scaled = fresh[m, pl.ds(r, size)] * inverse[m]
        at = pl.multiple_of(row_of(m, r, z), size)
        out[pl.ds(at, size)] = scaled.astype(jnp.bfloat16)

    for j in range(NPIECE):
        scale_own(1 + j * PIECE // ROWS, j * PIECE % ROWS, PIECE)
        if j > 0:
            send(("piece", j - 1, 1))
    scale_own(0, 0, ROWS)
    send(("piece", NPIECE - 1, 1))

    def hop(n, buf, at, axis, send_sem, recv_sem):
        slot, step = ((at, 1), (at, -1), (lax.rem(at + 3, 4), 1))[n]
        return pltpu.make_async_remote_copy(
            src_ref=buf.at[slot], dst_ref=buf.at[slot], send_sem=send_sem.at[n],
            recv_sem=recv_sem.at[n], device_id=beside(axis, at, step, 4), device_id_type=MESH,
        )

    low_x = (lowx, x, "width_1", lx_s, lx_r)
    gain_x = (norm_x, x, "width_1", nx_s, nx_r)
    gain_y = (norm_y, y, "width_0", ny_s, ny_r)

    def begin(*ring):
        hop(0, *ring).start()
        hop(1, *ring).start()

    def pass_on(*ring):
        hop(0, *ring).wait_recv()
        hop(2, *ring).start()
        hop(1, *ring).wait_recv()

    arrived("low", 0, 4)
    norm_x[x] = meta[:, 0, 3 * COLS :]
    begin(*low_x)
    begin(*gain_x)

    def scale_raw(back):
        o = lax.rem(z + back, Z)
        for b in range(NRAW):
            rows = pl.ds(b * BLOCK, BLOCK)
            block = fresh_of(lowx[b, o], high[0], rawx[o, rows])
            at = pl.multiple_of(row_of(0, b * BLOCK, o), BLOCK)
            out[pl.ds(at, BLOCK)] = (block * inverse[0]).astype(jnp.bfloat16)

    send(*raw(4, 0, 1, 2, 3))
    pass_on(*low_x)
    pass_on(*gain_x)
    send(("piece", 0, 2), ("piece", 1, 2))
    hop(2, *low_x).wait_recv()
    hop(2, *gain_x).wait_recv()
    norm_y[y] = jnp.sum(norm_x[...], axis=0)
    begin(*gain_y)
    scale_raw(1)
    scale_raw(7)
    send(("piece", 2, 2))
    pass_on(*gain_y)
    scale_raw(2)
    scale_raw(6)
    send(("piece", 3, 2))
    scale_raw(3)
    scale_raw(5)
    hop(2, *gain_y).wait_recv()
    for s in range(4):
        for t in range(Z):
            norm_all[pl.ds(t * 4 + s, 1)] = norm_y[s, pl.ds(t, 1)]
    norm[...] = norm_all[...].astype(jnp.bfloat16)
    send(("piece", 0, 3))
    for c in range(NRAW):
        arrived("raw", c, 4)
    scale_raw(4)
    send(*[("piece", j, 3) for j in range(1, NPIECE)])
    send(*[("piece", j, 4) for j in range(NPIECE)])
    for j in range(NPIECE):
        arrived("piece", j, 4)

    for item in sent:
        for copy in copies(*item):
            copy.wait_send()
    for ring in (low_x, gain_x, gain_y):
        for n in range(3):
            hop(n, *ring).wait_send()


def write_kernel(weights, fq, fk, fv, gain, sq, sk, sv, oq, ok, ov, og, sem):
    writes = [
        pltpu.make_async_copy(src, dst, sem.at[n])
        for n, (src, dst) in enumerate((
            (weights.at[pl.ds(0, WHOLE)], sq), (weights.at[pl.ds(WHOLE, WHOLE)], sk),
            (weights.at[pl.ds(2 * WHOLE, WHOLE)], sv), (fq, oq), (fk, ok), (fv, ov), (gain, og),
        ))
    ]
    for write in writes:
        write.start()
    for write in writes:
        write.wait()


def per_device(tq, lq, hq, tk, lk, hk, tv, lv, hv, nt, ns):
    hbm = pl.BlockSpec(memory_space=pltpu.HBM)
    vmem = pl.BlockSpec(memory_space=pltpu.VMEM)
    dma = pltpu.SemaphoreType.DMA
    f32, bf16 = jnp.float32, jnp.bfloat16
    args = (tq, lq.T, hq, tk, lk.T, hk, tv, lv.T, hv, nt.reshape(1, 32), ns.reshape(1, 32))
    gathered = pl.pallas_call(
        gather_kernel,
        name="gather_z",
        out_shape=(pltpu.VMEM((3 * WHOLE, COLS), bf16),)
        + (pltpu.VMEM((COLS,), f32),) * 3
        + (pltpu.VMEM((32, 128), bf16),),
        in_specs=[hbm] * 11,
        out_specs=(vmem,) * 5,
        scratch_shapes=[
            pltpu.VMEM((3, ROWS, COLS), bf16),
            pltpu.VMEM((3, 16, ROWS), bf16),
            pltpu.VMEM((3, 16, COLS), bf16),
            pltpu.VMEM((2, 1, 32), f32),
            pltpu.VMEM((3, ROWS, COLS), f32),
            pltpu.VMEM((Z, ROWS, COLS), bf16),
            pltpu.VMEM((4, Z, 16, BLOCK), bf16),
            pltpu.VMEM((Z, 1, META), f32),
            pltpu.VMEM((4, Z, 128), f32),
            pltpu.VMEM((4, Z, 128), f32),
            pltpu.VMEM((32, 128), f32),
            pltpu.VMEM((3, 1, COLS), f32),
            dma((12,)),
            dma((2, 4, NRAW)), dma((2, 4, NRAW)),
            dma((2, 4, NPIECE)), dma((2, 4, NPIECE)),
            dma((2, 4)), dma((2, 4)), dma((2, 4)), dma((2, 4)),
            dma((3,)), dma((3,)), dma((3,)), dma((3,)), dma((3,)), dma((3,)),
        ],
        compiler_params=pltpu.CompilerParams(
            collective_id=0, has_side_effects=True, vmem_limit_bytes=32 * 1024 * 1024
        ),
    )(*[pltpu.with_memory_space_constraint(a, pltpu.HBM) for a in args])
    shapes = ((WHOLE, COLS), bf16), ((COLS,), f32)
    sq, sk, sv, fq, fk, fv, gain = pl.pallas_call(
        write_kernel,
        name="write_out",
        out_shape=(jax.ShapeDtypeStruct(*shapes[0]),) * 3
        + (jax.ShapeDtypeStruct(*shapes[1]),) * 3
        + (jax.ShapeDtypeStruct((32, 128), bf16),),
        in_specs=[vmem] * 5,
        out_specs=(hbm,) * 7,
        scratch_shapes=[dma((7,))],
        compiler_params=pltpu.CompilerParams(vmem_limit_bytes=16 * 1024 * 1024),
    )(*gathered)
    return sq, sk, sv, fq, fk, fv, gain.reshape(4096)


def solution(mesh):
    finer = Mesh(
        mesh.devices.reshape(mesh.shape["zero"], 4, 4, mesh.shape["unit"]),
        ("zero", "width_0", "width_1", "unit"),
    )
    matrix, low, high = P(("unit", "zero"), WIDTH), P(("unit", "zero"), None), P("unit", WIDTH)
    return jax.shard_map(
        per_device,
        mesh=finer,
        in_specs=(matrix, low, high) * 3 + (P(UNIT_ZERO_WIDTH), P(UNIT_ZERO_WIDTH)),
        out_specs=(high, high, high, P(UNIT_WIDTH), P(UNIT_WIDTH), P(UNIT_WIDTH), P("unit")),
        check_vma=False,
    )
```

time: 93.5 us -> 74.4 us (0.80)
  Pallas kernels: 83.8 us -> 73.6 us
  local copies, waits for them, and re-layouts: 8.39 us -> 0 us
    pallas_call x1, Pallas kernels: 80.5 us -> 70.9 us  [per_device(): pl.pallas_call(gather_kernel, name='gather_z', out_shape=(pltpu.VMEM((3 *...]
    unnamed x22 -> x0, local copies, waits for them, and re-layouts: 8.39 us -> none
where the time goes in v2:
time: 74.4 us; the launch traced here: 74.3 us
  Pallas kernels  73.6 us (99%)
    pallas_call x1, Pallas kernels, per_device(): pl.pallas_call(gather_kernel, name='gather_z', out_shape=(pltpu.VMEM((3 *...  70.9 us
    pallas_call x1, Pallas kernels, per_device(): pl.pallas_call(write_kernel, name='write_out', out_shape=(jax.ShapeDtypeS...  2.77 us

profile of v2, /device:TPU:2, one launch (start us, length us, event | category | flops | bytes accessed | tf_op | source)
XLA Modules:
  0.0 74.3 jit_solution(6802558988211168118)
XLA Ops:
  0.6 70.9 %gather_z.1 = (bf16[12288,256]{1,0:T(8,128)(2,1)S(1)}, f32[256]{0:T(256)S(1)}, f32[256]{0:T(256)S(1)}, f32[256]{0:T(256)S(1)}, bf16[32,128]{1,0:T(8,128)(2,1)S(1)}) custom-call(bf16[512,256]{1,0:T(8,128)(2,1)} %tq.1, bf16[16,512]{1,0:T(8,128)(2,1)} %bitcast.6, bf16[16,256]{1,0:T(8,128)(2,1)} %hq.1, bf16[512,256]{1,0:T(8,128)(2,1)} %tk.1, ...), custom_call_target="tpu_custom_call" | custom-call | tf_op jit(solution)/shard_map/gather_z/pallas_call | solution.py:273
  71.5 2.8 %write_out.1 = (bf16[4096,256]{1,0:T(8,128)(2,1)}, bf16[4096,256]{1,0:T(8,128)(2,1)}, bf16[4096,256]{1,0:T(8,128)(2,1)}, f32[256]{0:T(256)}, f32[256]{0:T(256)}, /*index=5*/f32[256]{0:T(256)}, bf16[32,128]{1,0:T(8,128)(2,1)}) custom-call(bf16[12288,256]{1,0:T(8,128)(2,1)S(1)} %get-tuple-element.19.weights, f32[256]{0:T(256)S(1)} %get-tuple-element.20.fq, ...), custom_call_target="tpu_custom_call" | custom-call | tf_op jit(solution)/shard_map/write_out/pallas_call | solution.py:305

commit v3 on v2

--- a/solution.py
+++ b/solution.py
@@ -20,7 +20,7 @@
 COLS = 256
 WHOLE = Z * ROWS
 BLOCK = 128
-NRAW = ROWS // BLOCK
+NBLOCK = ROWS // BLOCK
 PIECE = 256
 NPIECE = 2 * ROWS // PIECE
 META = 3 * COLS + 128
@@ -38,7 +38,7 @@
     out, factor_q, factor_k, factor_v, norm,
     train, low, high, norm_in, fresh, rawx, lowx, meta, norm_x, norm_y, norm_all, inverse,
     load_sem, raw_s, raw_r, piece_s, piece_r, meta_s, meta_r, low_s, low_r,
-    lx_s, lx_r, nx_s, nx_r, ny_s, ny_r,
+    lx_s, lx_r, nx_s, nx_r, ny_s, ny_r, ready,
 ):
     z = lax.axis_index("zero")
     y = lax.axis_index("width_0")
@@ -62,13 +62,30 @@
 
     towards = (beside("zero", z, 1, Z), beside("zero", z, -1, Z))
     barrier = pltpu.get_barrier_semaphore()
-    neighbours = towards + (
-        beside("width_0", y, 1, 4), beside("width_0", y, -1, 4),
-        beside("width_1", x, 1, 4), beside("width_1", x, -1, 4),
-    )
-    for neighbour in neighbours:
+    for neighbour in towards:
         pl.semaphore_signal(barrier, inc=1, device_id=neighbour, device_id_type=MESH)
-    pl.semaphore_wait(barrier, len(neighbours))
+    plane = (("width_1", x), ("width_0", y))
+    for axis, at in plane:
+        @pl.when(at < 3)
+        def _(axis=axis, at=at):
+            pl.semaphore_signal(barrier, inc=1, device_id={axis: lax.rem(at + 1, 4)}, device_id_type=MESH)
+
+        @pl.when(at == 0)
+        def _(axis=axis, at=at):
+            pl.semaphore_signal(barrier, inc=1, device_id={axis: lax.rem(at + 3, 4)}, device_id_type=MESH)
+
+    lower = [(at + 1) // 2 for _, at in plane]
+    pl.semaphore_wait(barrier, 2 + lower[0] + lower[1])
+
+    def answer():
+        for n, (axis, at) in enumerate(plane):
+            @pl.when(at > 0)
+            def _(n=n, axis=axis, at=at):
+                pl.semaphore_signal(ready.at[n], inc=1, device_id={axis: lax.rem(at + 3, 4)}, device_id_type=MESH)
+
+            @pl.when(at == 3)
+            def _(n=n, axis=axis, at=at):
+                pl.semaphore_signal(ready.at[n], inc=1, device_id={axis: lax.rem(at + 1, 4)}, device_id_type=MESH)
 
     def origin(d, h):
         back = h - 1
@@ -80,64 +97,73 @@
             device_id=towards[d], device_id_type=MESH,
         )
 
-    def half(start, size, d, h):
-        return (start, size) if h < 4 else (start + d * (size // 2), size // 2)
-
-    def raw_copy(d, h, c):
-        at, size = half(c * BLOCK, BLOCK, d, h)
-        there = rawx.at[origin(d, h), pl.ds(at, size)]
-        here = train.at[0, pl.ds(at, size)] if h == 1 else there
-        return remote(here, there, raw_s.at[d, h - 1, c], raw_r.at[d, h - 1, c], d)
-
-    def low_copy(d, h):
+    def raw_copy(d, h, n):
+        size = BLOCK if h < 3 else 2 * BLOCK
+        rows = pl.ds((n if h < 4 else d) * size, size)
+        there = rawx.at[origin(d, h), rows]
+        here = train.at[0, rows] if h == 1 else there
+        return remote(here, there, raw_s.at[d, h - 1, n], raw_r.at[d, h - 1, n], d)
+
+    def low_copy(d, h, n):
         ref = lowx.at[x, origin(d, h)]
         return remote(ref, ref, low_s.at[d, h - 1], low_r.at[d, h - 1], d)
 
-    def meta_copy(d, h):
+    def meta_copy(d, h, n):
         ref = meta.at[origin(d, h)]
         return remote(ref, ref, meta_s.at[d, h - 1], meta_r.at[d, h - 1], d)
 
     def row_of(m, r, o):
         return m * WHOLE + o * ROWS + r
 
-    def piece_copy(d, h, j):
-        m, r = 1 + j * PIECE // ROWS, j * PIECE % ROWS
-        at, size = half(row_of(m, r, origin(d, h)), PIECE, d, h)
-        ref = out.at[pl.ds(pl.multiple_of(at, size), size)]
-        return remote(ref, ref, piece_s.at[d, h - 1, j], piece_r.at[d, h - 1, j], d)
-
-    def copies(kind, n, h):
-        if kind == "meta":
-            return [meta_copy(d, h) for d in ((0, 1) if h < 4 else (0,))]
-        if kind == "low":
-            return [low_copy(d, h) for d in ((0, 1) if h < 4 else (1,))]
-        return [(raw_copy if kind == "raw" else piece_copy)(d, h, n) for d in (0, 1)]
+    def piece_copy(d, h, n):
+        m, r = 1 + n * PIECE // ROWS, n * PIECE % ROWS
+        ref = out.at[pl.ds(pl.multiple_of(row_of(m, r, origin(d, h)), PIECE), PIECE)]
+        return remote(ref, ref, piece_s.at[d, h - 1, n], piece_r.at[d, h - 1, n], d)
+
+    copy_of = {"raw": raw_copy, "low": low_copy, "meta": meta_copy, "piece": piece_copy}
+
+    def goes(kind, n, h, d):
+        if h < 4 or kind == "raw":
+            return True
+        return {"low": d == 1, "meta": d == 0, "piece": n * 2 // NPIECE == d}[kind]
+
+    def needs(kind, n, h, d):
+        if h == 1:
+            return []
+        if kind == "raw" and h > 2:
+            return [(kind, 2 * n, 2), (kind, 2 * n + 1, 2)] if h == 3 else [(kind, d, 3)]
+        return [(kind, n, h - 1)]
 
     sent, landed = [], set()
 
+    def arrived_one(kind, n, h, d):
+        if goes(kind, n, h, d) and (kind, n, h, d) not in landed:
+            landed.add((kind, n, h, d))
+            copy_of[kind](d, h, n).wait_recv()
+
     def arrived(*item):
-        if item not in landed:
-            landed.add(item)
-            for copy in copies(*item):
-                copy.wait_recv()
+        for d in (0, 1):
+            arrived_one(*item, d)
 
     def send(*items):
         for kind, n, h in items:
-            if h > 1:
-                arrived(kind, n, h - 1)
-            for copy in copies(kind, n, h):
-                copy.start()
-            sent.append((kind, n, h))
+            for d in (0, 1):
+                if goes(kind, n, h, d):
+                    for before in needs(kind, n, h, d):
+                        arrived_one(*before, d)
+                    copy_of[kind](d, h, n).start()
+                    sent.append((kind, n, h, d))
 
     def raw(h, *pieces):
-        return [("raw", c, h) for c in pieces]
+        return [("raw", n, h) for n in pieces]
 
     def small(h):
         return [("low", 0, h), ("meta", 0, h)]
 
     loads[0].wait()
     loads[1].wait()
-    send(("raw", 0, 1), ("low", 0, 1), ("raw", 1, 1))
+    send(("raw", 0, 1), ("low", 0, 1))
+    answer()
     for load in loads[2:]:
         load.wait()
     for m in range(3):
@@ -154,10 +180,11 @@
     place = (lane == entry + 32 * x).astype(jnp.bfloat16)
     meta[z, :, pl.ds(3 * COLS, 128)] = jnp.dot(gain, place, preferred_element_type=jnp.float32)
 
-    send(("meta", 0, 1), *raw(1, 2, 3))
-    send(*small(2), *raw(2, 0, 1))
-    send(*small(3), *raw(2, 2, 3))
-    send(*small(4), *raw(3, 0, 1, 2, 3))
+    send(("meta", 0, 1), *raw(1, 1, 2))
+    send(*small(2), *raw(1, 3), *raw(2, 0))
+    send(*small(3), *raw(2, 1, 2))
+    send(*small(4), *raw(2, 3), *raw(3, 0))
+    arrived("meta", 0, 3)
     arrived("meta", 0, 4)
 
     top = jnp.max(meta[:, 0, : 3 * COLS], axis=0, keepdims=True)
@@ -176,7 +203,7 @@
         if j > 0:
             send(("piece", j - 1, 1))
     scale_own(0, 0, ROWS)
-    send(("piece", NPIECE - 1, 1))
+    send(("piece", NPIECE - 1, 1), *raw(3, 1))
 
     def hop(n, buf, at, axis, send_sem, recv_sem):
         slot, step = ((at, 1), (at, -1), (lax.rem(at + 3, 4), 1))[n]
@@ -198,20 +225,25 @@
         hop(2, *ring).start()
         hop(1, *ring).wait_recv()
 
+    arrived("low", 0, 3)
     arrived("low", 0, 4)
     norm_x[x] = meta[:, 0, 3 * COLS :]
+    for n, (_, at) in enumerate(plane):
+        @pl.when(at < 3)
+        def _(n=n):
+            pl.semaphore_wait(ready.at[n], 2 - lower[n])
     begin(*low_x)
     begin(*gain_x)
 
     def scale_raw(back):
         o = lax.rem(z + back, Z)
-        for b in range(NRAW):
+        for b in range(NBLOCK):
             rows = pl.ds(b * BLOCK, BLOCK)
             block = fresh_of(lowx[b, o], high[0], rawx[o, rows])
             at = pl.multiple_of(row_of(0, b * BLOCK, o), BLOCK)
             out[pl.ds(at, BLOCK)] = (block * inverse[0]).astype(jnp.bfloat16)
 
-    send(*raw(4, 0, 1, 2, 3))
+    send(*raw(4, 0))
     pass_on(*low_x)
     pass_on(*gain_x)
     send(("piece", 0, 2), ("piece", 1, 2))
@@ -226,6 +258,8 @@
     scale_raw(2)
     scale_raw(6)
     send(("piece", 3, 2))
+    arrived("raw", 0, 3)
+    arrived("raw", 1, 3)
     scale_raw(3)
     scale_raw(5)
     hop(2, *gain_y).wait_recv()
@@ -234,17 +268,17 @@
             norm_all[pl.ds(t * 4 + s, 1)] = norm_y[s, pl.ds(t, 1)]
     norm[...] = norm_all[...].astype(jnp.bfloat16)
     send(("piece", 0, 3))
-    for c in range(NRAW):
-        arrived("raw", c, 4)
+    arrived("raw", 0, 4)
     scale_raw(4)
-    send(*[("piece", j, 3) for j in range(1, NPIECE)])
-    send(*[("piece", j, 4) for j in range(NPIECE)])
-    for j in range(NPIECE):
-        arrived("piece", j, 4)
-
-    for item in sent:
-        for copy in copies(*item):
-            copy.wait_send()
+    send(*[("piece", n, 3) for n in range(1, NPIECE)])
+    send(*[("piece", n, 4) for n in range(NPIECE)])
+    for n in range(NPIECE):
+        arrived("piece", n, 3)
+    for n in range(NPIECE):
+        arrived("piece", n, 4)
+
+    for kind, n, h, d in sent:
+        copy_of[kind](d, h, n).wait_send()
     for ring in (low_x, gain_x, gain_y):
         for n in range(3):
             hop(n, *ring).wait_send()
@@ -292,10 +326,11 @@
             pltpu.VMEM((32, 128), f32),
             pltpu.VMEM((3, 1, COLS), f32),
             dma((12,)),
-            dma((2, 4, NRAW)), dma((2, 4, NRAW)),
+            dma((2, 4, NBLOCK)), dma((2, 4, NBLOCK)),
             dma((2, 4, NPIECE)), dma((2, 4, NPIECE)),
             dma((2, 4)), dma((2, 4)), dma((2, 4)), dma((2, 4)),
             dma((3,)), dma((3,)), dma((3,)), dma((3,)), dma((3,)), dma((3,)),
+            pltpu.SemaphoreType.REGULAR((2,)),
         ],
         compiler_params=pltpu.CompilerParams(
             collective_id=0, has_side_effects=True, vmem_limit_bytes=32 * 1024 * 1024

time: 74.4 us -> 73.1 us (0.983)
  Pallas kernels: 73.6 us -> 72.4 us
    pallas_call x1, Pallas kernels: 70.9 us -> 69.6 us  [per_device(): pl.pallas_call(gather_kernel, name='gather_z', out_shape=(pltpu.VMEM((3 *...]
where the time goes in v3:
time: 73.1 us; the launch traced here: 73 us
  Pallas kernels  72.4 us (99%)
    pallas_call x1, Pallas kernels, per_device(): pl.pallas_call(gather_kernel, name='gather_z', out_shape=(pltpu.VMEM((3 *...  69.6 us
    pallas_call x1, Pallas kernels, per_device(): pl.pallas_call(write_kernel, name='write_out', out_shape=(jax.ShapeDtypeS...  2.77 us

profile of v3, /device:TPU:2, one launch (start us, length us, event | category | flops | bytes accessed | tf_op | source)
XLA Modules:
  0.0 73.0 jit_solution(6415579967793587551)
XLA Ops:
  0.6 69.6 %gather_z.1 = (bf16[12288,256]{1,0:T(8,128)(2,1)S(1)}, f32[256]{0:T(256)S(1)}, f32[256]{0:T(256)S(1)}, f32[256]{0:T(256)S(1)}, bf16[32,128]{1,0:T(8,128)(2,1)S(1)}) custom-call(bf16[512,256]{1,0:T(8,128)(2,1)} %tq.1, bf16[16,512]{1,0:T(8,128)(2,1)} %bitcast.6, bf16[16,256]{1,0:T(8,128)(2,1)} %hq.1, bf16[512,256]{1,0:T(8,128)(2,1)} %tk.1, ...), custom_call_target="tpu_custom_call" | custom-call | tf_op jit(solution)/shard_map/gather_z/pallas_call | solution.py:307
  70.2 2.8 %write_out.1 = (bf16[4096,256]{1,0:T(8,128)(2,1)}, bf16[4096,256]{1,0:T(8,128)(2,1)}, bf16[4096,256]{1,0:T(8,128)(2,1)}, f32[256]{0:T(256)}, f32[256]{0:T(256)}, /*index=5*/f32[256]{0:T(256)}, bf16[32,128]{1,0:T(8,128)(2,1)}) custom-call(bf16[12288,256]{1,0:T(8,128)(2,1)S(1)} %get-tuple-element.19.weights, f32[256]{0:T(256)S(1)} %get-tuple-element.20.fq, ...), custom_call_target="tpu_custom_call" | custom-call | tf_op jit(solution)/shard_map/write_out/pallas_call | solution.py:340

commit v4 on v3

--- a/solution.py
+++ b/solution.py
@@ -24,6 +24,7 @@
 PIECE = 256
 NPIECE = 2 * ROWS // PIECE
 META = 3 * COLS + 128
+RAW, SCALED, LOW, TOP, LOW_X, NORM_X, NORM_Y = range(7)
 
 
 def fresh_of(low_t, high, train):
@@ -37,25 +38,27 @@
     tq, lq, hq, tk, lk, hk, tv, lv, hv, nt, ns,
     out, factor_q, factor_k, factor_v, norm,
     train, low, high, norm_in, fresh, rawx, lowx, meta, norm_x, norm_y, norm_all, inverse,
-    load_sem, raw_s, raw_r, piece_s, piece_r, meta_s, meta_r, low_s, low_r,
-    lx_s, lx_r, nx_s, nx_r, ny_s, ny_r, ready,
+    load_sem, sends, raw_r, piece_r, meta_r, low_r, last, lx_r, nx_r, ny_r, ready,
 ):
     z = lax.axis_index("zero")
     y = lax.axis_index("width_0")
     x = lax.axis_index("width_1")
 
     lanes = pl.ds(pl.multiple_of(x * BLOCK, BLOCK), BLOCK)
-    loads = [
-        pltpu.make_async_copy(src, dst, load_sem.at[n])
-        for n, (src, dst) in enumerate((
-            (tq, train.at[0]), (lq.at[:, lanes], lowx.at[x, z]), (lq, low.at[0]), (hq, high.at[0]),
-            (tk, train.at[1]), (lk, low.at[1]), (hk, high.at[1]),
-            (tv, train.at[2]), (lv, low.at[2]), (hv, high.at[2]),
-            (nt, norm_in.at[0]), (ns, norm_in.at[1]),
-        ))
-    ]
-    for load in loads:
-        load.start()
+    groups = (
+        ((tq, train.at[0]),),
+        ((lq.at[:, lanes], lowx.at[x, z]),),
+        ((tk, train.at[1]), (tv, train.at[2])),
+        ((lq, low.at[0]), (lk, low.at[1]), (lv, low.at[2])),
+        ((hq, high.at[0]), (hk, high.at[1]), (hv, high.at[2])),
+        ((nt, norm_in.at[0]), (ns, norm_in.at[1])),
+    )
+    for n, group in enumerate(groups):
+        for src, dst in group:
+            pltpu.make_async_copy(src, dst, load_sem.at[n]).start()
+
+    def all_of(ref, sem):
+        pltpu.make_async_copy(ref, ref, sem).wait()
 
     def beside(axis, at, step, size):
         return {axis: lax.rem(at + (step + size), size)}
@@ -91,81 +94,79 @@
         back = h - 1
         return lax.rem(z + (Z - back if d == 0 else back), Z)
 
-    def remote(src, dst, send, recv, d):
+    def remote(src, dst, kind, recv, d):
         return pltpu.make_async_remote_copy(
-            src_ref=src, dst_ref=dst, send_sem=send, recv_sem=recv,
+            src_ref=src, dst_ref=dst, send_sem=sends.at[kind], recv_sem=recv,
             device_id=towards[d], device_id_type=MESH,
         )
 
+    def half(start, size, d, h):
+        return (start, size) if h < 4 else (start + d * (size // 2), size // 2)
+
     def raw_copy(d, h, n):
-        size = BLOCK if h < 3 else 2 * BLOCK
-        rows = pl.ds((n if h < 4 else d) * size, size)
-        there = rawx.at[origin(d, h), rows]
-        here = train.at[0, rows] if h == 1 else there
-        return remote(here, there, raw_s.at[d, h - 1, n], raw_r.at[d, h - 1, n], d)
+        at, size = half(n * BLOCK, BLOCK, d, h)
+        there = rawx.at[origin(d, h), pl.ds(at, size)]
+        here = train.at[0, pl.ds(at, size)] if h == 1 else there
+        recv = raw_r.at[d, h - 1, n] if h < 4 else last.at[RAW]
+        return remote(here, there, RAW, recv, d)
 
     def low_copy(d, h, n):
         ref = lowx.at[x, origin(d, h)]
-        return remote(ref, ref, low_s.at[d, h - 1], low_r.at[d, h - 1], d)
+        recv = last.at[LOW] if ends(LOW, d, h) else low_r.at[d, h - 1]
+        return remote(ref, ref, LOW, recv, d)
 
     def meta_copy(d, h, n):
         ref = meta.at[origin(d, h)]
-        return remote(ref, ref, meta_s.at[d, h - 1], meta_r.at[d, h - 1], d)
+        recv = last.at[TOP] if ends(TOP, d, h) else meta_r.at[1 - d, h - 1]
+        return remote(ref, ref, TOP, recv, d)
 
     def row_of(m, r, o):
         return m * WHOLE + o * ROWS + r
 
     def piece_copy(d, h, n):
         m, r = 1 + n * PIECE // ROWS, n * PIECE % ROWS
-        ref = out.at[pl.ds(pl.multiple_of(row_of(m, r, origin(d, h)), PIECE), PIECE)]
-        return remote(ref, ref, piece_s.at[d, h - 1, n], piece_r.at[d, h - 1, n], d)
-
-    copy_of = {"raw": raw_copy, "low": low_copy, "meta": meta_copy, "piece": piece_copy}
-
-    def goes(kind, n, h, d):
-        if h < 4 or kind == "raw":
-            return True
-        return {"low": d == 1, "meta": d == 0, "piece": n * 2 // NPIECE == d}[kind]
-
-    def needs(kind, n, h, d):
-        if h == 1:
-            return []
-        if kind == "raw" and h > 2:
-            return [(kind, 2 * n, 2), (kind, 2 * n + 1, 2)] if h == 3 else [(kind, d, 3)]
-        return [(kind, n, h - 1)]
-
-    sent, landed = [], set()
+        at, size = half(row_of(m, r, origin(d, h)), PIECE, d, h)
+        ref = out.at[pl.ds(pl.multiple_of(at, size), size)]
+        recv = piece_r.at[d, h - 1, n] if h < 4 else last.at[SCALED]
+        return remote(ref, ref, SCALED, recv, d)
+
+    copy_of = (raw_copy, piece_copy, low_copy, meta_copy)
+
+    def goes(kind, h, d):
+        return h < 4 or kind in (RAW, SCALED) or d == (1 if kind == LOW else 0)
+
+    def ends(kind, d, h):
+        return not goes(kind, h + 1, d) if h < 4 else True
+
+    landed = set()
 
     def arrived_one(kind, n, h, d):
-        if goes(kind, n, h, d) and (kind, n, h, d) not in landed:
+        if (kind, n, h, d) not in landed and not ends(kind, d, h):
             landed.add((kind, n, h, d))
             copy_of[kind](d, h, n).wait_recv()
-
-    def arrived(*item):
-        for d in (0, 1):
-            arrived_one(*item, d)
 
     def send(*items):
         for kind, n, h in items:
             for d in (0, 1):
-                if goes(kind, n, h, d):
-                    for before in needs(kind, n, h, d):
-                        arrived_one(*before, d)
+                if h > 1:
+                    arrived_one(kind, n, h - 1, d)
+                if goes(kind, h, d):
                     copy_of[kind](d, h, n).start()
-                    sent.append((kind, n, h, d))
 
     def raw(h, *pieces):
-        return [("raw", n, h) for n in pieces]
+        return [(RAW, n, h) for n in pieces]
 
     def small(h):
-        return [("low", 0, h), ("meta", 0, h)]
-
-    loads[0].wait()
-    loads[1].wait()
-    send(("raw", 0, 1), ("low", 0, 1))
+        return [(LOW, 0, h), (TOP, 0, h)]
+
+    all_of(train.at[0], load_sem.at[0])
+    all_of(lowx.at[x, z], load_sem.at[1])
+    send(*raw(1, 0, 1))
     answer()
-    for load in loads[2:]:
-        load.wait()
+    all_of(train.at[pl.ds(1, 2)], load_sem.at[2])
+    all_of(low, load_sem.at[3])
+    all_of(high, load_sem.at[4])
+    all_of(norm_in, load_sem.at[5])
     for m in range(3):
         top = jnp.zeros((8, COLS), jnp.float32)
         for b in range(ROWS // BLOCK):
@@ -180,12 +181,11 @@
     place = (lane == entry + 32 * x).astype(jnp.bfloat16)
     meta[z, :, pl.ds(3 * COLS, 128)] = jnp.dot(gain, place, preferred_element_type=jnp.float32)
 
-    send(("meta", 0, 1), *raw(1, 1, 2))
-    send(*small(2), *raw(1, 3), *raw(2, 0))
-    send(*small(3), *raw(2, 1, 2))
-    send(*small(4), *raw(2, 3), *raw(3, 0))
-    arrived("meta", 0, 3)
-    arrived("meta", 0, 4)
+    send(*small(1), *raw(1, 2, 3), *raw(2, 0))
+    send(*small(2), *raw(2, 1, 2))
+    send(*small(3), *raw(2, 3), *raw(3, 0, 1))
+    send(*small(4), *raw(3, 2, 3), *raw(4, 0))
+    all_of(meta.at[pl.ds(0, 2)], last.at[TOP])
 
     top = jnp.max(meta[:, 0, : 3 * COLS], axis=0, keepdims=True)
     for m, factor in enumerate((factor_q, factor_k, factor_v)):
@@ -201,20 +201,20 @@
     for j in range(NPIECE):
         scale_own(1 + j * PIECE // ROWS, j * PIECE % ROWS, PIECE)
         if j > 0:
-            send(("piece", j - 1, 1))
+            send((SCALED, j - 1, 1))
     scale_own(0, 0, ROWS)
-    send(("piece", NPIECE - 1, 1), *raw(3, 1))
-
-    def hop(n, buf, at, axis, send_sem, recv_sem):
+    send((SCALED, NPIECE - 1, 1))
+
+    def hop(n, buf, at, axis, kind, recv):
         slot, step = ((at, 1), (at, -1), (lax.rem(at + 3, 4), 1))[n]
         return pltpu.make_async_remote_copy(
-            src_ref=buf.at[slot], dst_ref=buf.at[slot], send_sem=send_sem.at[n],
-            recv_sem=recv_sem.at[n], device_id=beside(axis, at, step, 4), device_id_type=MESH,
+            src_ref=buf.at[slot], dst_ref=buf.at[slot], send_sem=sends.at[kind],
+            recv_sem=recv.at[0 if n == 0 else 1], device_id=beside(axis, at, step, 4), device_id_type=MESH,
         )
 
-    low_x = (lowx, x, "width_1", lx_s, lx_r)
-    gain_x = (norm_x, x, "width_1", nx_s, nx_r)
-    gain_y = (norm_y, y, "width_0", ny_s, ny_r)
+    low_x = (lowx, x, "width_1", LOW_X, lx_r)
+    gain_x = (norm_x, x, "width_1", NORM_X, nx_r)
+    gain_y = (norm_y, y, "width_0", NORM_Y, ny_r)
 
     def begin(*ring):
         hop(0, *ring).start()
@@ -223,10 +223,11 @@
     def pass_on(*ring):
         hop(0, *ring).wait_recv()
         hop(2, *ring).start()
-        hop(1, *ring).wait_recv()
-
-    arrived("low", 0, 3)
-    arrived("low", 0, 4)
+
+    def complete(buf, at, axis, kind, recv):
+        all_of(buf.at[pl.ds(0, 2)], recv.at[1])
+
+    all_of(lowx.at[0, pl.ds(0, 2)], last.at[LOW])
     norm_x[x] = meta[:, 0, 3 * COLS :]
     for n, (_, at) in enumerate(plane):
         @pl.when(at < 3)
@@ -243,45 +244,42 @@
             at = pl.multiple_of(row_of(0, b * BLOCK, o), BLOCK)
             out[pl.ds(at, BLOCK)] = (block * inverse[0]).astype(jnp.bfloat16)
 
-    send(*raw(4, 0))
+    send(*raw(4, 1, 2, 3))
     pass_on(*low_x)
     pass_on(*gain_x)
-    send(("piece", 0, 2), ("piece", 1, 2))
-    hop(2, *low_x).wait_recv()
-    hop(2, *gain_x).wait_recv()
+    send((SCALED, 0, 2), (SCALED, 1, 2))
+    complete(*low_x)
+    complete(*gain_x)
     norm_y[y] = jnp.sum(norm_x[...], axis=0)
     begin(*gain_y)
     scale_raw(1)
     scale_raw(7)
-    send(("piece", 2, 2))
+    send((SCALED, 2, 2))
     pass_on(*gain_y)
     scale_raw(2)
     scale_raw(6)
-    send(("piece", 3, 2))
-    arrived("raw", 0, 3)
-    arrived("raw", 1, 3)
+    send((SCALED, 3, 2))
     scale_raw(3)
     scale_raw(5)
-    hop(2, *gain_y).wait_recv()
+    complete(*gain_y)
     for s in range(4):
         for t in range(Z):
             norm_all[pl.ds(t * 4 + s, 1)] = norm_y[s, pl.ds(t, 1)]
     norm[...] = norm_all[...].astype(jnp.bfloat16)
-    send(("piece", 0, 3))
-    arrived("raw", 0, 4)
+    send((SCALED, 0, 3))
+    all_of(rawx.at[0], last.at[RAW])
     scale_raw(4)
-    send(*[("piece", n, 3) for n in range(1, NPIECE)])
-    send(*[("piece", n, 4) for n in range(NPIECE)])
-    for n in range(NPIECE):
-        arrived("piece", n, 3)
-    for n in range(NPIECE):
-        arrived("piece", n, 4)
-
-    for kind, n, h, d in sent:
-        copy_of[kind](d, h, n).wait_send()
-    for ring in (low_x, gain_x, gain_y):
-        for n in range(3):
-            hop(n, *ring).wait_send()
+    send(*[(SCALED, n, 3) for n in range(1, NPIECE)])
+    send(*[(SCALED, n, 4) for n in range(NPIECE)])
+    all_of(out.at[pl.ds(0, 2 * ROWS)], last.at[SCALED])
+
+    all_of(out.at[pl.ds(0, 7 * ROWS)], sends.at[RAW])
+    all_of(out.at[pl.ds(0, 14 * ROWS)], sends.at[SCALED])
+    all_of(lowx.at[0, pl.ds(0, 7)], sends.at[LOW])
+    all_of(meta.at[pl.ds(0, 7)], sends.at[TOP])
+    all_of(lowx.at[pl.ds(0, 3)], sends.at[LOW_X])
+    all_of(norm_x.at[pl.ds(0, 3)], sends.at[NORM_X])
+    all_of(norm_y.at[pl.ds(0, 3)], sends.at[NORM_Y])
 
 
 def write_kernel(weights, fq, fk, fv, gain, sq, sk, sv, oq, ok, ov, og, sem):
@@ -325,11 +323,9 @@
             pltpu.VMEM((4, Z, 128), f32),
             pltpu.VMEM((32, 128), f32),
             pltpu.VMEM((3, 1, COLS), f32),
-            dma((12,)),
-            dma((2, 4, NBLOCK)), dma((2, 4, NBLOCK)),
-            dma((2, 4, NPIECE)), dma((2, 4, NPIECE)),
-            dma((2, 4)), dma((2, 4)), dma((2, 4)), dma((2, 4)),
-            dma((3,)), dma((3,)), dma((3,)), dma((3,)), dma((3,)), dma((3,)),
+            dma((6,)), dma((7,)),
+            dma((2, 3, NBLOCK)), dma((2, 3, NPIECE)), dma((2, 3)), dma((2, 3)), dma((4,)),
+            dma((2,)), dma((2,)), dma((2,)),
             pltpu.SemaphoreType.REGULAR((2,)),
         ],
         compiler_params=pltpu.CompilerParams(

time: 73.1 us -> 71.3 us (0.975)
  Pallas kernels: 72.4 us -> 70.6 us
    pallas_call x1, Pallas kernels: 69.6 us -> 67.8 us  [per_device(): pl.pallas_call(gather_kernel, name='gather_z', out_shape=(pltpu.VMEM((3 *...]
where the time goes in v4:
time: 71.3 us; the launch traced here: 71.2 us
  Pallas kernels  70.6 us (99%)
    pallas_call x1, Pallas kernels, per_device(): pl.pallas_call(gather_kernel, name='gather_z', out_shape=(pltpu.VMEM((3 *...  67.8 us
    pallas_call x1, Pallas kernels, per_device(): pl.pallas_call(write_kernel, name='write_out', out_shape=(jax.ShapeDtypeS...  2.77 us

profile of v4, /device:TPU:2, one launch (start us, length us, event | category | flops | bytes accessed | tf_op | source)
XLA Modules:
  0.0 71.2 jit_solution(16839472033718414232)
XLA Ops:
  0.6 67.8 %gather_z.1 = (bf16[12288,256]{1,0:T(8,128)(2,1)S(1)}, f32[256]{0:T(256)S(1)}, f32[256]{0:T(256)S(1)}, f32[256]{0:T(256)S(1)}, bf16[32,128]{1,0:T(8,128)(2,1)S(1)}) custom-call(bf16[512,256]{1,0:T(8,128)(2,1)} %tq.1, bf16[16,512]{1,0:T(8,128)(2,1)} %bitcast.6, bf16[16,256]{1,0:T(8,128)(2,1)} %hq.1, bf16[512,256]{1,0:T(8,128)(2,1)} %tk.1, ...), custom_call_target="tpu_custom_call" | custom-call | tf_op jit(solution)/shard_map/gather_z/pallas_call | solution.py:305
  68.5 2.8 %write_out.1 = (bf16[4096,256]{1,0:T(8,128)(2,1)}, bf16[4096,256]{1,0:T(8,128)(2,1)}, bf16[4096,256]{1,0:T(8,128)(2,1)}, f32[256]{0:T(256)}, f32[256]{0:T(256)}, /*index=5*/f32[256]{0:T(256)}, bf16[32,128]{1,0:T(8,128)(2,1)}) custom-call(bf16[12288,256]{1,0:T(8,128)(2,1)S(1)} %get-tuple-element.19.weights, f32[256]{0:T(256)S(1)} %get-tuple-element.20.fq, ...), custom_call_target="tpu_custom_call" | custom-call | tf_op jit(solution)/shard_map/write_out/pallas_call | solution.py:336

commit v5 on v4

--- a/solution.py
+++ b/solution.py
@@ -24,7 +24,7 @@
 PIECE = 256
 NPIECE = 2 * ROWS // PIECE
 META = 3 * COLS + 128
-RAW, SCALED, LOW, TOP, LOW_X, NORM_X, NORM_Y = range(7)
+RAW, SCALED, LOW, TOP, LOW_X, NORM_X, NORM_Y, MOVED = range(8)
 
 
 def fresh_of(low_t, high, train):
@@ -65,8 +65,12 @@
 
     towards = (beside("zero", z, 1, Z), beside("zero", z, -1, Z))
     barrier = pltpu.get_barrier_semaphore()
-    for neighbour in towards:
-        pl.semaphore_signal(barrier, inc=1, device_id=neighbour, device_id_type=MESH)
+    pl.semaphore_signal(barrier, inc=1, device_id=towards[1], device_id_type=MESH)
+
+    @pl.when(z < Z - 1)
+    def _():
+        pl.semaphore_signal(barrier, inc=1, device_id=towards[0], device_id_type=MESH)
+
     plane = (("width_1", x), ("width_0", y))
     for axis, at in plane:
         @pl.when(at < 3)
@@ -78,7 +82,11 @@
             pl.semaphore_signal(barrier, inc=1, device_id={axis: lax.rem(at + 3, 4)}, device_id_type=MESH)
 
     lower = [(at + 1) // 2 for _, at in plane]
-    pl.semaphore_wait(barrier, 2 + lower[0] + lower[1])
+    pl.semaphore_wait(barrier, 1 + lax.min(z, 1) + lower[0] + lower[1])
+
+    @pl.when(z == Z - 1)
+    def _():
+        pl.semaphore_signal(ready.at[2], inc=1, device_id=towards[0], device_id_type=MESH)
 
     def answer():
         for n, (axis, at) in enumerate(plane):
@@ -123,12 +131,12 @@
     def row_of(m, r, o):
         return m * WHOLE + o * ROWS + r
 
-    def piece_copy(d, h, n):
+    def piece_copy(d, h, n, kind=SCALED, part=None):
         m, r = 1 + n * PIECE // ROWS, n * PIECE % ROWS
-        at, size = half(row_of(m, r, origin(d, h)), PIECE, d, h)
+        at, size = half(row_of(m, r, origin(d, h)), PIECE, d if part is None else part, h)
         ref = out.at[pl.ds(pl.multiple_of(at, size), size)]
         recv = piece_r.at[d, h - 1, n] if h < 4 else last.at[SCALED]
-        return remote(ref, ref, SCALED, recv, d)
+        return remote(ref, ref, kind, recv, d)
 
     copy_of = (raw_copy, piece_copy, low_copy, meta_copy)
 
@@ -161,7 +169,15 @@
 
     all_of(train.at[0], load_sem.at[0])
     all_of(lowx.at[x, z], load_sem.at[1])
-    send(*raw(1, 0, 1))
+    raw_copy(0, 1, 0).start()
+    raw_copy(0, 1, 1).start()
+
+    @pl.when(z == 0)
+    def _():
+        pl.semaphore_wait(ready.at[2], 1)
+
+    raw_copy(1, 1, 0).start()
+    raw_copy(1, 1, 1).start()
     answer()
     all_of(train.at[pl.ds(1, 2)], load_sem.at[2])
     all_of(low, load_sem.at[3])
@@ -270,11 +286,35 @@
     all_of(rawx.at[0], last.at[RAW])
     scale_raw(4)
     send(*[(SCALED, n, 3) for n in range(1, NPIECE)])
-    send(*[(SCALED, n, 4) for n in range(NPIECE)])
+
+    end = 0
+    for d in (0, 1):
+        arrived_one(SCALED, end, 3, d)
+    piece_copy(1, 4, end).start()
+    usual, moved = piece_copy(0, 4, end, MOVED), piece_copy(1, 4, end, MOVED, 0)
+
+    @pl.when(z < Z - 1)
+    def _():
+        usual.start()
+
+    @pl.when(z == 1)
+    def _():
+        moved.start()
+
+    send(*[(SCALED, n, 4) for n in range(1, NPIECE)])
     all_of(out.at[pl.ds(0, 2 * ROWS)], last.at[SCALED])
 
     all_of(out.at[pl.ds(0, 7 * ROWS)], sends.at[RAW])
-    all_of(out.at[pl.ds(0, 14 * ROWS)], sends.at[SCALED])
+    all_of(out.at[pl.ds(0, 14 * ROWS - PIECE // 2)], sends.at[SCALED])
+
+    @pl.when(jnp.logical_and(z != 1, z < Z - 1))
+    def _():
+        usual.wait_send()
+
+    @pl.when(z == 1)
+    def _():
+        all_of(out.at[pl.ds(0, PIECE)], sends.at[MOVED])
+
     all_of(lowx.at[0, pl.ds(0, 7)], sends.at[LOW])
     all_of(meta.at[pl.ds(0, 7)], sends.at[TOP])
     all_of(lowx.at[pl.ds(0, 3)], sends.at[LOW_X])
@@ -323,10 +363,10 @@
             pltpu.VMEM((4, Z, 128), f32),
             pltpu.VMEM((32, 128), f32),
             pltpu.VMEM((3, 1, COLS), f32),
-            dma((6,)), dma((7,)),
+            dma((6,)), dma((8,)),
             dma((2, 3, NBLOCK)), dma((2, 3, NPIECE)), dma((2, 3)), dma((2, 3)), dma((4,)),
             dma((2,)), dma((2,)), dma((2,)),
-            pltpu.SemaphoreType.REGULAR((2,)),
+            pltpu.SemaphoreType.REGULAR((3,)),
         ],
         compiler_params=pltpu.CompilerParams(
             collective_id=0, has_side_effects=True, vmem_limit_bytes=32 * 1024 * 1024

time: 71.3 us -> 70.7 us (level)
  no operation moved by 1% of the time
where the time goes in v5:
time: 70.7 us; the launch traced here: 70.6 us
  Pallas kernels  69.9 us (99%)
    pallas_call x1, Pallas kernels, per_device(): pl.pallas_call(gather_kernel, name='gather_z', out_shape=(pltpu.VMEM((3 *...  67.1 us
    pallas_call x1, Pallas kernels, per_device(): pl.pallas_call(write_kernel, name='write_out', out_shape=(jax.ShapeDtypeS...  2.77 us

profile of v5, /device:TPU:2, one launch (start us, length us, event | category | flops | bytes accessed | tf_op | source)
XLA Modules:
  0.0 70.6 jit_solution(10627556542771654655)
XLA Ops:
  0.6 67.1 %gather_z.1 = (bf16[12288,256]{1,0:T(8,128)(2,1)S(1)}, f32[256]{0:T(256)S(1)}, f32[256]{0:T(256)S(1)}, f32[256]{0:T(256)S(1)}, bf16[32,128]{1,0:T(8,128)(2,1)S(1)}) custom-call(bf16[512,256]{1,0:T(8,128)(2,1)} %tq.1, bf16[16,512]{1,0:T(8,128)(2,1)} %bitcast.6, bf16[16,256]{1,0:T(8,128)(2,1)} %hq.1, bf16[512,256]{1,0:T(8,128)(2,1)} %tk.1, ...), custom_call_target="tpu_custom_call" | custom-call | tf_op jit(solution)/shard_map/gather_z/pallas_call | solution.py:345
  67.8 2.8 %write_out.1 = (bf16[4096,256]{1,0:T(8,128)(2,1)}, bf16[4096,256]{1,0:T(8,128)(2,1)}, bf16[4096,256]{1,0:T(8,128)(2,1)}, f32[256]{0:T(256)}, f32[256]{0:T(256)}, /*index=5*/f32[256]{0:T(256)}, bf16[32,128]{1,0:T(8,128)(2,1)}) custom-call(bf16[12288,256]{1,0:T(8,128)(2,1)S(1)} %get-tuple-element.19.weights, f32[256]{0:T(256)S(1)} %get-tuple-element.20.fq, ...), custom_call_target="tpu_custom_call" | custom-call | tf_op jit(solution)/shard_map/write_out/pallas_call | solution.py:376

commit v6 on v5

--- a/solution.py
+++ b/solution.py
@@ -21,10 +21,11 @@
 WHOLE = Z * ROWS
 BLOCK = 128
 NBLOCK = ROWS // BLOCK
+PIECES = ((1, 0, 512), (2, 0, 256), (2, 256, 256))
+NPIECE = len(PIECES)
 PIECE = 256
-NPIECE = 2 * ROWS // PIECE
-META = 3 * COLS + 128
-RAW, SCALED, LOW, TOP, LOW_X, NORM_X, NORM_Y, MOVED = range(8)
+META = 1024
+RAW, SCALED, LOW, TOP, MOVED = range(5)
 
 
 def fresh_of(low_t, high, train):
@@ -38,7 +39,7 @@
     tq, lq, hq, tk, lk, hk, tv, lv, hv, nt, ns,
     out, factor_q, factor_k, factor_v, norm,
     train, low, high, norm_in, fresh, rawx, lowx, meta, norm_x, norm_y, norm_all, inverse,
-    load_sem, sends, raw_r, piece_r, meta_r, low_r, last, lx_r, nx_r, ny_r, ready,
+    load_sem, sends, arrivals, meta_r, low_r, low_last, x_r, y_r, ready,
 ):
     z = lax.axis_index("zero")
     y = lax.axis_index("width_0")
@@ -47,10 +48,10 @@
     lanes = pl.ds(pl.multiple_of(x * BLOCK, BLOCK), BLOCK)
     groups = (
         ((tq, train.at[0]),),
-        ((lq.at[:, lanes], lowx.at[x, z]),),
-        ((tk, train.at[1]), (tv, train.at[2])),
-        ((lq, low.at[0]), (lk, low.at[1]), (lv, low.at[2])),
-        ((hq, high.at[0]), (hk, high.at[1]), (hv, high.at[2])),
+        (
+            (tk, train.at[1]), (tv, train.at[2]), (lq, low.at[0]), (lk, low.at[1]), (lv, low.at[2]),
+            (hq, high.at[0]), (hk, high.at[1]), (hv, high.at[2]), (lq.at[:, lanes], lowx.at[x, z]),
+        ),
         ((nt, norm_in.at[0]), (ns, norm_in.at[1])),
     )
     for n, group in enumerate(groups):
@@ -104,7 +105,7 @@
 
     def remote(src, dst, kind, recv, d):
         return pltpu.make_async_remote_copy(
-            src_ref=src, dst_ref=dst, send_sem=sends.at[kind], recv_sem=recv,
+            src_ref=src, dst_ref=dst, send_sem=sends.at[kind // MOVED], recv_sem=recv,
             device_id=towards[d], device_id_type=MESH,
         )
 
@@ -115,27 +116,27 @@
         at, size = half(n * BLOCK, BLOCK, d, h)
         there = rawx.at[origin(d, h), pl.ds(at, size)]
         here = train.at[0, pl.ds(at, size)] if h == 1 else there
-        recv = raw_r.at[d, h - 1, n] if h < 4 else last.at[RAW]
+        recv = arrivals.at[d, h - 1, n] if h < 4 else load_sem.at[1]
         return remote(here, there, RAW, recv, d)
 
     def low_copy(d, h, n):
         ref = lowx.at[x, origin(d, h)]
-        recv = last.at[LOW] if ends(LOW, d, h) else low_r.at[d, h - 1]
+        recv = low_last if ends(LOW, d, h) else low_r.at[2 * h - 1 - d]
         return remote(ref, ref, LOW, recv, d)
 
     def meta_copy(d, h, n):
         ref = meta.at[origin(d, h)]
-        recv = last.at[TOP] if ends(TOP, d, h) else meta_r.at[1 - d, h - 1]
+        recv = load_sem.at[2] if ends(TOP, d, h) else meta_r.at[2 * h - 2 + d]
         return remote(ref, ref, TOP, recv, d)
 
     def row_of(m, r, o):
         return m * WHOLE + o * ROWS + r
 
     def piece_copy(d, h, n, kind=SCALED, part=None):
-        m, r = 1 + n * PIECE // ROWS, n * PIECE % ROWS
-        at, size = half(row_of(m, r, origin(d, h)), PIECE, d if part is None else part, h)
+        m, r, size = PIECES[n]
+        at, size = half(row_of(m, r, origin(d, h)), size, d if part is None else part, h)
         ref = out.at[pl.ds(pl.multiple_of(at, size), size)]
-        recv = piece_r.at[d, h - 1, n] if h < 4 else last.at[SCALED]
+        recv = arrivals.at[d, h - 1, n] if h < 4 else load_sem.at[0]
         return remote(ref, ref, kind, recv, d)
 
     copy_of = (raw_copy, piece_copy, low_copy, meta_copy)
@@ -168,7 +169,6 @@
         return [(LOW, 0, h), (TOP, 0, h)]
 
     all_of(train.at[0], load_sem.at[0])
-    all_of(lowx.at[x, z], load_sem.at[1])
     raw_copy(0, 1, 0).start()
     raw_copy(0, 1, 1).start()
 
@@ -179,10 +179,8 @@
     raw_copy(1, 1, 0).start()
     raw_copy(1, 1, 1).start()
     answer()
-    all_of(train.at[pl.ds(1, 2)], load_sem.at[2])
-    all_of(low, load_sem.at[3])
-    all_of(high, load_sem.at[4])
-    all_of(norm_in, load_sem.at[5])
+    all_of(out.at[pl.ds(0, 2 * ROWS + 152)], load_sem.at[1])
+    all_of(norm_in, load_sem.at[2])
     for m in range(3):
         top = jnp.zeros((8, COLS), jnp.float32)
         for b in range(ROWS // BLOCK):
@@ -201,7 +199,7 @@
     send(*small(2), *raw(2, 1, 2))
     send(*small(3), *raw(2, 3), *raw(3, 0, 1))
     send(*small(4), *raw(3, 2, 3), *raw(4, 0))
-    all_of(meta.at[pl.ds(0, 2)], last.at[TOP])
+    all_of(meta.at[pl.ds(0, 2)], load_sem.at[2])
 
     top = jnp.max(meta[:, 0, : 3 * COLS], axis=0, keepdims=True)
     for m, factor in enumerate((factor_q, factor_k, factor_v)):
@@ -215,36 +213,40 @@
         out[pl.ds(at, size)] = scaled.astype(jnp.bfloat16)
 
     for j in range(NPIECE):
-        scale_own(1 + j * PIECE // ROWS, j * PIECE % ROWS, PIECE)
+        scale_own(*PIECES[j])
         if j > 0:
             send((SCALED, j - 1, 1))
     scale_own(0, 0, ROWS)
     send((SCALED, NPIECE - 1, 1))
 
-    def hop(n, buf, at, axis, kind, recv):
+    def hop(n, buf, at, axis, recv):
         slot, step = ((at, 1), (at, -1), (lax.rem(at + 3, 4), 1))[n]
         return pltpu.make_async_remote_copy(
-            src_ref=buf.at[slot], dst_ref=buf.at[slot], send_sem=sends.at[kind],
+            src_ref=buf.at[slot], dst_ref=buf.at[slot], send_sem=sends.at[0],
             recv_sem=recv.at[0 if n == 0 else 1], device_id=beside(axis, at, step, 4), device_id_type=MESH,
         )
 
-    low_x = (lowx, x, "width_1", LOW_X, lx_r)
-    gain_x = (norm_x, x, "width_1", NORM_X, nx_r)
-    gain_y = (norm_y, y, "width_0", NORM_Y, ny_r)
+    low_x = (lowx, x, "width_1", x_r)
+    gain_x = (norm_x, x, "width_1", x_r)
+    gain_y = (norm_y, y, "width_0", y_r)
 
     def begin(*ring):
         hop(0, *ring).start()
         hop(1, *ring).start()
 
-    def pass_on(*ring):
-        hop(0, *ring).wait_recv()
-        hop(2, *ring).start()
-
-    def complete(buf, at, axis, kind, recv):
-        all_of(buf.at[pl.ds(0, 2)], recv.at[1])
-
-    all_of(lowx.at[0, pl.ds(0, 2)], last.at[LOW])
-    norm_x[x] = meta[:, 0, 3 * COLS :]
+    def sizes(n, *rings):
+        return out.at[pl.ds(0, n * sum(8 if ring[0] is not lowx else 64 for ring in rings))]
+
+    def pass_on(*rings):
+        all_of(sizes(1, *rings), rings[0][-1].at[0])
+        for ring in rings:
+            hop(2, *ring).start()
+
+    def complete(*rings):
+        all_of(sizes(2, *rings), rings[0][-1].at[1])
+
+    all_of(lowx.at[0, pl.ds(0, 2)], low_last)
+    norm_x[x] = meta[:, 0, 3 * COLS : 3 * COLS + 128]
     for n, (_, at) in enumerate(plane):
         @pl.when(at < 3)
         def _(n=n):
@@ -261,33 +263,31 @@
             out[pl.ds(at, BLOCK)] = (block * inverse[0]).astype(jnp.bfloat16)
 
     send(*raw(4, 1, 2, 3))
-    pass_on(*low_x)
-    pass_on(*gain_x)
+    pass_on(low_x, gain_x)
     send((SCALED, 0, 2), (SCALED, 1, 2))
-    complete(*low_x)
-    complete(*gain_x)
+    complete(low_x, gain_x)
     norm_y[y] = jnp.sum(norm_x[...], axis=0)
     begin(*gain_y)
     scale_raw(1)
     scale_raw(7)
-    send((SCALED, 2, 2))
-    pass_on(*gain_y)
+    pass_on(gain_y)
     scale_raw(2)
     scale_raw(6)
-    send((SCALED, 3, 2))
+    send((SCALED, 2, 2))
     scale_raw(3)
     scale_raw(5)
-    complete(*gain_y)
+    complete(gain_y)
     for s in range(4):
         for t in range(Z):
             norm_all[pl.ds(t * 4 + s, 1)] = norm_y[s, pl.ds(t, 1)]
     norm[...] = norm_all[...].astype(jnp.bfloat16)
     send((SCALED, 0, 3))
-    all_of(rawx.at[0], last.at[RAW])
+    all_of(rawx.at[0], load_sem.at[1])
     scale_raw(4)
     send(*[(SCALED, n, 3) for n in range(1, NPIECE)])
 
-    end = 0
+    send((SCALED, 0, 4))
+    end = 1
     for d in (0, 1):
         arrived_one(SCALED, end, 3, d)
     piece_copy(1, 4, end).start()
@@ -301,11 +301,10 @@
     def _():
         moved.start()
 
-    send(*[(SCALED, n, 4) for n in range(1, NPIECE)])
-    all_of(out.at[pl.ds(0, 2 * ROWS)], last.at[SCALED])
-
-    all_of(out.at[pl.ds(0, 7 * ROWS)], sends.at[RAW])
-    all_of(out.at[pl.ds(0, 14 * ROWS - PIECE // 2)], sends.at[SCALED])
+    send((SCALED, 2, 4))
+    all_of(out.at[pl.ds(0, 2 * ROWS)], load_sem.at[0])
+
+    all_of(out.at[pl.ds(0, 21 * ROWS - PIECE // 2 + 14 * 8 + 3 * (64 + 8 + 8))], sends.at[0])
 
     @pl.when(jnp.logical_and(z != 1, z < Z - 1))
     def _():
@@ -313,13 +312,7 @@
 
     @pl.when(z == 1)
     def _():
-        all_of(out.at[pl.ds(0, PIECE)], sends.at[MOVED])
-
-    all_of(lowx.at[0, pl.ds(0, 7)], sends.at[LOW])
-    all_of(meta.at[pl.ds(0, 7)], sends.at[TOP])
-    all_of(lowx.at[pl.ds(0, 3)], sends.at[LOW_X])
-    all_of(norm_x.at[pl.ds(0, 3)], sends.at[NORM_X])
-    all_of(norm_y.at[pl.ds(0, 3)], sends.at[NORM_Y])
+        all_of(out.at[pl.ds(0, PIECE)], sends.at[1])
 
 
 def write_kernel(weights, fq, fk, fv, gain, sq, sk, sv, oq, ok, ov, og, sem):
@@ -363,9 +356,9 @@
             pltpu.VMEM((4, Z, 128), f32),
             pltpu.VMEM((32, 128), f32),
             pltpu.VMEM((3, 1, COLS), f32),
-            dma((6,)), dma((8,)),
-            dma((2, 3, NBLOCK)), dma((2, 3, NPIECE)), dma((2, 3)), dma((2, 3)), dma((4,)),
-            dma((2,)), dma((2,)), dma((2,)),
+            dma((3,)), dma((2,)),
+            dma((2, 3, NBLOCK)), dma((5,)), dma((5,)), dma,
+            dma((2,)), dma((2,)),
             pltpu.SemaphoreType.REGULAR((3,)),
         ],
         compiler_params=pltpu.CompilerParams(

time: 70.7 us -> 70.3 us (level)
  no operation moved by 1% of the time
where the time goes in v6:
time: 70.3 us; the launch traced here: 70.2 us
  Pallas kernels  69.6 us (99%)
    pallas_call x1, Pallas kernels, per_device(): pl.pallas_call(gather_kernel, name='gather_z', out_shape=(pltpu.VMEM((3 *...  66.8 us
    pallas_call x1, Pallas kernels, per_device(): pl.pallas_call(write_kernel, name='write_out', out_shape=(jax.ShapeDtypeS...  2.77 us

profile of v6, /device:TPU:2, one launch (start us, length us, event | category | flops | bytes accessed | tf_op | source)
XLA Modules:
  0.0 70.2 jit_solution(15029415885743487261)
XLA Ops:
  0.6 66.8 %gather_z.1 = (bf16[12288,256]{1,0:T(8,128)(2,1)S(1)}, f32[256]{0:T(256)S(1)}, f32[256]{0:T(256)S(1)}, f32[256]{0:T(256)S(1)}, bf16[32,128]{1,0:T(8,128)(2,1)S(1)}) custom-call(bf16[512,256]{1,0:T(8,128)(2,1)} %tq.1, bf16[16,512]{1,0:T(8,128)(2,1)} %bitcast.6, bf16[16,256]{1,0:T(8,128)(2,1)} %hq.1, bf16[512,256]{1,0:T(8,128)(2,1)} %tk.1, ...), custom_call_target="tpu_custom_call" | custom-call | tf_op jit(solution)/shard_map/gather_z/pallas_call | solution.py:338
  67.4 2.8 %write_out.1 = (bf16[4096,256]{1,0:T(8,128)(2,1)}, bf16[4096,256]{1,0:T(8,128)(2,1)}, bf16[4096,256]{1,0:T(8,128)(2,1)}, f32[256]{0:T(256)}, f32[256]{0:T(256)}, /*index=5*/f32[256]{0:T(256)}, bf16[32,128]{1,0:T(8,128)(2,1)}) custom-call(bf16[12288,256]{1,0:T(8,128)(2,1)S(1)} %get-tuple-element.19.weights, f32[256]{0:T(256)S(1)} %get-tuple-element.20.fq, ...), custom_call_target="tpu_custom_call" | custom-call | tf_op jit(solution)/shard_map/write_out/pallas_call | solution.py:369

commit v7 on v6

--- a/solution.py
+++ b/solution.py
@@ -169,15 +169,23 @@
         return [(LOW, 0, h), (TOP, 0, h)]
 
     all_of(train.at[0], load_sem.at[0])
-    raw_copy(0, 1, 0).start()
-    raw_copy(0, 1, 1).start()
-
-    @pl.when(z == 0)
-    def _():
-        pl.semaphore_wait(ready.at[2], 1)
-
-    raw_copy(1, 1, 0).start()
-    raw_copy(1, 1, 1).start()
+    def first():
+        raw_copy(0, 1, 0).start()
+        raw_copy(0, 1, 1).start()
+
+        @pl.when(z == 0)
+        def _():
+            pl.semaphore_wait(ready.at[2], 1)
+
+        raw_copy(1, 1, 0).start()
+        raw_copy(1, 1, 1).start()
+
+    unit = lax.axis_index("unit")
+
+    @pl.when(unit == 0)
+    def _():
+        first()
+
     answer()
     all_of(out.at[pl.ds(0, 2 * ROWS + 152)], load_sem.at[1])
     all_of(norm_in, load_sem.at[2])
@@ -194,6 +202,10 @@
     entry = lax.broadcasted_iota(jnp.int32, (32, 128), 0)
     place = (lane == entry + 32 * x).astype(jnp.bfloat16)
     meta[z, :, pl.ds(3 * COLS, 128)] = jnp.dot(gain, place, preferred_element_type=jnp.float32)
+
+    @pl.when(unit == 1)
+    def _():
+        first()
 
     send(*small(1), *raw(1, 2, 3), *raw(2, 0))
     send(*small(2), *raw(2, 1, 2))

time: 70.3 us -> 70.2 us (level)
  no operation moved by 1% of the time
where the time goes in v7:
time: 70.2 us; the launch traced here: 70.1 us
  Pallas kernels  69.5 us (99%)
    pallas_call x1, Pallas kernels, per_device(): pl.pallas_call(gather_kernel, name='gather_z', out_shape=(pltpu.VMEM((3 *...  66.7 us
    pallas_call x1, Pallas kernels, per_device(): pl.pallas_call(write_kernel, name='write_out', out_shape=(jax.ShapeDtypeS...  2.77 us

profile of v7, /device:TPU:2, one launch (start us, length us, event | category | flops | bytes accessed | tf_op | source)
XLA Modules:
  0.0 70.1 jit_solution(14403131573174595132)
XLA Ops:
  0.6 66.7 %gather_z.1 = (bf16[12288,256]{1,0:T(8,128)(2,1)S(1)}, f32[256]{0:T(256)S(1)}, f32[256]{0:T(256)S(1)}, f32[256]{0:T(256)S(1)}, bf16[32,128]{1,0:T(8,128)(2,1)S(1)}) custom-call(bf16[512,256]{1,0:T(8,128)(2,1)} %tq.1, bf16[16,512]{1,0:T(8,128)(2,1)} %bitcast.6, bf16[16,256]{1,0:T(8,128)(2,1)} %hq.1, bf16[512,256]{1,0:T(8,128)(2,1)} %tk.1, ...), custom_call_target="tpu_custom_call" | custom-call | tf_op jit(solution)/shard_map/gather_z/pallas_call | solution.py:350
  67.4 2.8 %write_out.1 = (bf16[4096,256]{1,0:T(8,128)(2,1)}, bf16[4096,256]{1,0:T(8,128)(2,1)}, bf16[4096,256]{1,0:T(8,128)(2,1)}, f32[256]{0:T(256)}, f32[256]{0:T(256)}, /*index=5*/f32[256]{0:T(256)}, bf16[32,128]{1,0:T(8,128)(2,1)}) custom-call(bf16[12288,256]{1,0:T(8,128)(2,1)S(1)} %get-tuple-element.19.weights, f32[256]{0:T(256)S(1)} %get-tuple-element.20.fq, ...), custom_call_target="tpu_custom_call" | custom-call | tf_op jit(solution)/shard_map/write_out/pallas_call | solution.py:381

commit v8 on v6

--- a/solution.py
+++ b/solution.py
@@ -21,9 +21,9 @@
 WHOLE = Z * ROWS
 BLOCK = 128
 NBLOCK = ROWS // BLOCK
-PIECES = ((1, 0, 512), (2, 0, 256), (2, 256, 256))
+PIECES = ((1, 0, 512), (2, 0, 320), (2, 320, 192))
 NPIECE = len(PIECES)
-PIECE = 256
+PIECE = 320
 META = 1024
 RAW, SCALED, LOW, TOP, MOVED = range(5)
 
@@ -135,7 +135,7 @@
     def piece_copy(d, h, n, kind=SCALED, part=None):
         m, r, size = PIECES[n]
         at, size = half(row_of(m, r, origin(d, h)), size, d if part is None else part, h)
-        ref = out.at[pl.ds(pl.multiple_of(at, size), size)]
+        ref = out.at[pl.ds(pl.multiple_of(at, 32), size)]
         recv = arrivals.at[d, h - 1, n] if h < 4 else load_sem.at[0]
         return remote(ref, ref, kind, recv, d)
 
@@ -209,7 +209,7 @@
 
     def scale_own(m, r, size):
         scaled = fresh[m, pl.ds(r, size)] * inverse[m]
-        at = pl.multiple_of(row_of(m, r, z), size)
+        at = pl.multiple_of(row_of(m, r, z), 32)
         out[pl.ds(at, size)] = scaled.astype(jnp.bfloat16)
 
     for j in range(NPIECE):

time: 70.3 us -> 70.2 us (level)
  no operation moved by 1% of the time
where the time goes in v8:
time: 70.2 us; the launch traced here: 70.1 us
  Pallas kernels  69.4 us (99%)
    pallas_call x1, Pallas kernels, per_device(): pl.pallas_call(gather_kernel, name='gather_z', out_shape=(pltpu.VMEM((3 *...  66.7 us
    pallas_call x1, Pallas kernels, per_device(): pl.pallas_call(write_kernel, name='write_out', out_shape=(jax.ShapeDtypeS...  2.77 us

profile of v8, /device:TPU:2, one launch (start us, length us, event | category | flops | bytes accessed | tf_op | source)
XLA Modules:
  0.0 70.1 jit_solution(5480023090362430692)
XLA Ops:
  0.6 66.7 %gather_z.1 = (bf16[12288,256]{1,0:T(8,128)(2,1)S(1)}, f32[256]{0:T(256)S(1)}, f32[256]{0:T(256)S(1)}, f32[256]{0:T(256)S(1)}, bf16[32,128]{1,0:T(8,128)(2,1)S(1)}) custom-call(bf16[512,256]{1,0:T(8,128)(2,1)} %tq.1, bf16[16,512]{1,0:T(8,128)(2,1)} %bitcast.6, bf16[16,256]{1,0:T(8,128)(2,1)} %hq.1, bf16[512,256]{1,0:T(8,128)(2,1)} %tk.1, ...), custom_call_target="tpu_custom_call" | custom-call | tf_op jit(solution)/shard_map/gather_z/pallas_call | solution.py:338
  67.3 2.8 %write_out.1 = (bf16[4096,256]{1,0:T(8,128)(2,1)}, bf16[4096,256]{1,0:T(8,128)(2,1)}, bf16[4096,256]{1,0:T(8,128)(2,1)}, f32[256]{0:T(256)}, f32[256]{0:T(256)}, /*index=5*/f32[256]{0:T(256)}, bf16[32,128]{1,0:T(8,128)(2,1)}) custom-call(bf16[12288,256]{1,0:T(8,128)(2,1)S(1)} %get-tuple-element.19.weights, f32[256]{0:T(256)S(1)} %get-tuple-element.20.fq, ...), custom_call_target="tpu_custom_call" | custom-call | tf_op jit(solution)/shard_map/write_out/pallas_call | solution.py:369

commit v9 on v8

--- a/solution.py
+++ b/solution.py
@@ -24,7 +24,7 @@
 PIECES = ((1, 0, 512), (2, 0, 320), (2, 320, 192))
 NPIECE = len(PIECES)
 PIECE = 320
-META = 1024
+META = 3 * COLS + 128
 RAW, SCALED, LOW, TOP, MOVED = range(5)
 
 
@@ -105,7 +105,7 @@
 
     def remote(src, dst, kind, recv, d):
         return pltpu.make_async_remote_copy(
-            src_ref=src, dst_ref=dst, send_sem=sends.at[kind // MOVED], recv_sem=recv,
+            src_ref=src, dst_ref=dst, send_sem=sends.at[2 if kind == TOP else kind // MOVED], recv_sem=recv,
             device_id=towards[d], device_id_type=MESH,
         )
 
@@ -304,7 +304,8 @@
     send((SCALED, 2, 4))
     all_of(out.at[pl.ds(0, 2 * ROWS)], load_sem.at[0])
 
-    all_of(out.at[pl.ds(0, 21 * ROWS - PIECE // 2 + 14 * 8 + 3 * (64 + 8 + 8))], sends.at[0])
+    all_of(out.at[pl.ds(0, 21 * ROWS - PIECE // 2 + 7 * 8 + 3 * (64 + 8 + 8))], sends.at[0])
+    all_of(meta.at[pl.ds(0, 7)], sends.at[2])
 
     @pl.when(jnp.logical_and(z != 1, z < Z - 1))
     def _():
@@ -316,17 +317,17 @@
 
 
 def write_kernel(weights, fq, fk, fv, gain, sq, sk, sv, oq, ok, ov, og, sem):
-    writes = [
-        pltpu.make_async_copy(src, dst, sem.at[n])
-        for n, (src, dst) in enumerate((
-            (weights.at[pl.ds(0, WHOLE)], sq), (weights.at[pl.ds(WHOLE, WHOLE)], sk),
-            (weights.at[pl.ds(2 * WHOLE, WHOLE)], sv), (fq, oq), (fk, ok), (fv, ov), (gain, og),
-        ))
+    for m, dst in enumerate((sq, sk, sv)):
+        pltpu.make_async_copy(weights.at[pl.ds(m * WHOLE, WHOLE)], dst, sem.at[0]).start()
+    rest = [
+        pltpu.make_async_copy(src, dst, sem.at[1 + n])
+        for n, (src, dst) in enumerate(((fq, oq), (fk, ok), (fv, ov), (gain, og)))
     ]
-    for write in writes:
+    for write in rest:
         write.start()
-    for write in writes:
+    for write in rest:
         write.wait()
+    pltpu.make_async_copy(weights, weights, sem.at[0]).wait()
 
 
 def per_device(tq, lq, hq, tk, lk, hk, tv, lv, hv, nt, ns):
@@ -356,7 +357,7 @@
             pltpu.VMEM((4, Z, 128), f32),
             pltpu.VMEM((32, 128), f32),
             pltpu.VMEM((3, 1, COLS), f32),
-            dma((3,)), dma((2,)),
+            dma((3,)), dma((3,)),
             dma((2, 3, NBLOCK)), dma((5,)), dma((5,)), dma,
             dma((2,)), dma((2,)),
             pltpu.SemaphoreType.REGULAR((3,)),
@@ -374,7 +375,7 @@
         + (jax.ShapeDtypeStruct((32, 128), bf16),),
         in_specs=[vmem] * 5,
         out_specs=(hbm,) * 7,
-        scratch_shapes=[dma((7,))],
+        scratch_shapes=[dma((5,))],
         compiler_params=pltpu.CompilerParams(vmem_limit_bytes=16 * 1024 * 1024),
     )(*gathered)
     return sq, sk, sv, fq, fk, fv, gain.reshape(4096)

time: 70.2 us -> 70.1 us (level)
  no operation moved by 1% of the time
where the time goes in v9:
time: 70.1 us; the launch traced here: 70 us
  Pallas kernels  69.4 us (99%)
    pallas_call x1, Pallas kernels, per_device(): pl.pallas_call(gather_kernel, name='gather_z', out_shape=(pltpu.VMEM((3 *...  66.7 us
    pallas_call x1, Pallas kernels, per_device(): pl.pallas_call(write_kernel, name='write_out', out_shape=(jax.ShapeDtypeS...  2.75 us

profile of v9, /device:TPU:2, one launch (start us, length us, event | category | flops | bytes accessed | tf_op | source)
XLA Modules:
  0.0 70.0 jit_solution(6653247480237483898)
XLA Ops:
  0.6 66.7 %gather_z.1 = (bf16[12288,256]{1,0:T(8,128)(2,1)S(1)}, f32[256]{0:T(256)S(1)}, f32[256]{0:T(256)S(1)}, f32[256]{0:T(256)S(1)}, bf16[32,128]{1,0:T(8,128)(2,1)S(1)}) custom-call(bf16[512,256]{1,0:T(8,128)(2,1)} %tq.1, bf16[16,512]{1,0:T(8,128)(2,1)} %bitcast.6, bf16[16,256]{1,0:T(8,128)(2,1)} %hq.1, bf16[512,256]{1,0:T(8,128)(2,1)} %tk.1, ...), custom_call_target="tpu_custom_call" | custom-call | tf_op jit(solution)/shard_map/gather_z/pallas_call | solution.py:339
  67.3 2.7 %write_out.1 = (bf16[4096,256]{1,0:T(8,128)(2,1)}, bf16[4096,256]{1,0:T(8,128)(2,1)}, bf16[4096,256]{1,0:T(8,128)(2,1)}, f32[256]{0:T(256)}, f32[256]{0:T(256)}, /*index=5*/f32[256]{0:T(256)}, bf16[32,128]{1,0:T(8,128)(2,1)}) custom-call(bf16[12288,256]{1,0:T(8,128)(2,1)S(1)} %get-tuple-element.19.weights, f32[256]{0:T(256)S(1)} %get-tuple-element.20.fq, ...), custom_call_target="tpu_custom_call" | custom-call | tf_op jit(solution)/shard_map/write_out/pallas_call | solution.py:370
